TPU v7x, 256 devices: a whole 4x4x8 slice. The times are simulated.
256 devices in a mesh: tile: 32 (over y, z), lat: 4 (over x), emu: 2 (over core).
Axes of the slice: x: 4, y: 4, z: 8, core: 2. Of those that a mesh axis runs over, the one named last changes fastest.
Arguments:
- state: float32 [512, 128, 12, 128], P('tile', ('lat', 'emu')), may hold values from -6 to 6
- diffusivity: float32 [12, 128], replicated, may hold values from 0.03 to 0.2
- wind: float32 [512, 128], P('tile', ('lat', 'emu')), may hold values from -0.5 to 0.5
- land_mask: int32 [512, 128], P('tile', ('lat', 'emu')), may hold values 0 or 1
- routes: int32 [32, 4, 2, 256, 1], P('tile', 'lat', 'emu'), may hold values from 0 to 127; in each aligned block of 256 rows (0 to 255, 256 to 511, ..., all dimensions but the last counted through in order) at most 2 rows name the same one
- counts: int32 [32, 4, 2], P('tile', 'lat', 'emu'), may hold values from 64 to 256
- w_in: bfloat16 [128, 1536, 1024], P(('tile', 'lat')), may hold values from -0.15625 to 0.15625
- b_in: float32 [128, 1024], P(('tile', 'lat')), may hold values from -3 to 3
- land_vec: float32 [128, 1024], P(('tile', 'lat')), may hold values from -5 to 5
- w_hid: bfloat16 [128, 2, 1024, 1024], P(('tile', 'lat')), may hold values from -0.1875 to 0.1875
- b_hid: float32 [128, 2, 1024], P(('tile', 'lat')), may hold values from -3 to 3
- w_out: bfloat16 [128, 1024, 512], P(('tile', 'lat')), may hold values from -0.1875 to 0.1875
Outputs:
- updated: float32 [512, 128, 4, 128], P('tile', ('lat', 'emu'))
Inputs may be any that keep to these rules, and one draw needn't show every extreme that they name: `routes`: among the 256 columns of one device, at most 2 name the same expert.
All inputs are finite; a program needn't handle non-finite values. No bound on the sum of `land_mask` on one device may be relied on, other than what follows from the above.
Results may differ from a plain program's by a relative error of at most 0.0026.
Values may be sent and summed in bfloat16 or wider, within the bound.
A program may use at most 64 MiB of HBM per device.

v0:
```python
import jax
import jax.numpy as jnp
from jax import lax
from jax.sharding import PartitionSpec as P


def extended(block, sides, width, periodic):
    for axis, dim in sides:
        count = lax.axis_size(axis)
        forward = [(i, i + 1) for i in range(count - 1)]
        if periodic:
            forward.append((count - 1, 0))
        backward = [(target, source) for source, target in forward]
        low = lax.ppermute(
            lax.slice_in_dim(block, block.shape[dim] - width, None, axis=dim), axis, forward
        )
        high = lax.ppermute(lax.slice_in_dim(block, 0, width, axis=dim), axis, backward)
        block = jnp.concatenate([low, block, high], axis=dim)
    return block


def advance(center, east, west, north, south, diffusivity, wind):
    spread = east + west + north + south - 4.0 * center
    return center + diffusivity[None, None] * spread - 0.5 * wind[:, :, None, None] * (east - west)


def column_slots(route_flat, count, experts, capacity):
    columns = route_flat.shape[0]
    positions = jnp.arange(columns, dtype=jnp.int32)
    active = positions < count
    onehot = (
        (route_flat[:, None] == jnp.arange(experts, dtype=jnp.int32)[None, :]) & active[:, None]
    ).astype(jnp.int32)
    before = jnp.cumsum(onehot, axis=0) - onehot
    ranking = jnp.sum(before * onehot, axis=1)
    slot_index = jnp.where(active, route_flat * capacity + ranking, experts * capacity)
    return (slot_index, active)


def run_network(features, flags, w_first, b_first, land_add, w_inner, b_inner, w_last):
    lead = features.shape[:-1]
    rows = features.reshape(-1, features.shape[-1])
    pre = jnp.dot(rows, w_first, preferred_element_type=jnp.float32) + b_first[None, :]
    pre = pre + flags.reshape(-1, 1).astype(jnp.float32) * land_add[None, :]
    hidden = jax.nn.silu(pre).astype(jnp.bfloat16)
    for number in range(w_inner.shape[0]):
        inner = (
            jnp.dot(hidden, w_inner[number], preferred_element_type=jnp.float32)
            + b_inner[number][None, :]
        )
        hidden = jax.nn.silu(inner).astype(jnp.bfloat16)
    produced = jnp.dot(hidden, w_last, preferred_element_type=jnp.float32).astype(jnp.bfloat16)
    return produced.reshape(lead + (w_last.shape[1],))


def body(
    state, diffusivity, wind, land_mask, routes, counts, w_in, b_in, land_vec, w_hid, b_hid, w_out
):
    lon_cells, lat_cells, variables, levels = state.shape
    lon_ext = extended(state, (("tile", 0),), 1, True)
    lat_ext = extended(state, ((("lat", "emu"), 1),), 1, False)
    advanced = advance(
        state, lon_ext[2:], lon_ext[:-2], lat_ext[:, 2:], lat_ext[:, :-2], diffusivity, wind
    )
    columns = lon_cells * lat_cells
    fsize = variables * levels
    outf = w_out.shape[2]
    out_vars = outf // levels
    tiles = lax.axis_size("tile")
    bands = lax.axis_size("lat")
    experts = tiles * bands
    capacity = max(2, columns * 5 // (4 * experts))
    features = advanced.astype(jnp.bfloat16).reshape(columns, fsize)
    slot_index, active = column_slots(
        routes.reshape(columns), counts.reshape(()), experts, capacity
    )
    outbound = jnp.zeros((experts * capacity + 1, fsize), jnp.bfloat16).at[slot_index].set(features)
    outbound = outbound[:-1].reshape(experts, capacity, fsize)
    land_rows = land_mask.reshape(columns, 1).astype(jnp.bfloat16)
    flags = jnp.zeros((experts * capacity + 1, 1), jnp.bfloat16).at[slot_index].set(land_rows)
    flags = flags[:-1].reshape(experts, capacity, 1)
    produced = run_network(
        lax.all_to_all(outbound, ("tile", "lat"), split_axis=0, concat_axis=0, tiled=True),
        lax.all_to_all(flags, ("tile", "lat"), split_axis=0, concat_axis=0, tiled=True),
        w_in[0],
        b_in[0],
        land_vec[0],
        w_hid[0],
        b_hid[0],
        w_out[0],
    )
    returned = lax.all_to_all(produced, ("tile", "lat"), split_axis=0, concat_axis=0, tiled=True)
    flat = jnp.concatenate([returned.reshape(-1, outf), jnp.zeros((1, outf), jnp.bfloat16)], axis=0)
    tendency = flat[slot_index].astype(jnp.float32)
    return advanced[:, :, :out_vars, :] + tendency.reshape(lon_cells, lat_cells, out_vars, levels)


def solution(mesh):
    in_specs = (
        P("tile", ("lat", "emu"), None, None),
        P(),
        P("tile", ("lat", "emu")),
        P("tile", ("lat", "emu")),
        P("tile", "lat", "emu", None, None),
        P("tile", "lat", "emu"),
        P(("tile", "lat"), None, None),
        P(("tile", "lat"), None),
        P(("tile", "lat"), None),
        P(("tile", "lat"), None, None, None),
        P(("tile", "lat"), None, None),
        P(("tile", "lat"), None, None),
    )
    out_specs = P("tile", ("lat", "emu"), None, None)
    return jax.shard_map(body, mesh=mesh, in_specs=in_specs, out_specs=out_specs, check_vma=False)
```

profile of v0, /device:TPU:1, one launch (start us, length us, event | category | flops | bytes accessed | tf_op | source)
XLA Modules:
  0.0 124.4 jit_solution(2248665939664039405)
XLA Ops:
  0.0 0.0 copy-start
  0.0 0.0 copy-start.2
  0.0 0.0 copy-start.4
  0.0 0.0 copy-start.5
  0.0 0.0 copy-start.3
  0.0 2.1 %copy.45 = f32[16,16,12,128]{3,2,1,0:T(8,128)S(1)} copy(f32[16,16,12,128]{3,1,2,0:T(8,128)} %param.12) | data formatting | bytes 3145728 | tf_op args[0]
  2.1 0.0 copy-start.1
  2.1 0.8 fusion.60
  2.9 8.8 %collective-permute-start = (f32[1,16,12,128]{3,2,1,0:T(8,128)}, f32[1,16,12,128]{3,2,1,0:T(8,128)S(1)}, u32[]{:S(2)}, u32[]{:S(2)}) collective-permute-start(f32[1,16,12,128]{3,2,1,0:T(8,128)} %get-tuple-element.7), channel_id=1, source_target_pairs={{8,0},{16,8},{24,16},{32,24},{40,32},{48,40},{56,48},{64,56},{72,6... | collective-permute-start | bytes 294920 | tf_op jit(solution)/shard_map/ppermute | solution.py:17
  11.7 0.0 collective-permute-start.1
  11.7 0.0 copy-done.1
  11.7 0.7 fusion.61
  12.5 2.9 %collective-permute-start.2 = (f32[16,1,12,128]{3,2,1,0:T(8,128)}, f32[16,1,12,128]{3,2,1,0:T(8,128)}, u32[]{:S(2)}, u32[]{:S(2)}) collective-permute-start(f32[16,1,12,128]{3,2,1,0:T(8,128)} %get-tuple-element.9), channel_id=1, source_target_pairs={{1,0},{2,1},{3,2},{4,3},{5,4},{6,5},{7,6},{9,8},{10,9},{11,10},{12... | collective-permute-start | bytes 294920 | tf_op jit(solution)/shard_map/ppermute | solution.py:17
  15.3 3.0 %collective-permute-start.3 = (f32[16,1,12,128]{3,2,1,0:T(8,128)}, f32[16,1,12,128]{3,2,1,0:T(8,128)}, u32[]{:S(2)}, u32[]{:S(2)}) collective-permute-start(f32[16,1,12,128]{3,2,1,0:T(8,128)} %get-tuple-element.10), channel_id=1, source_target_pairs={{0,1},{1,2},{2,3},{3,4},{4,5},{5,6},{6,7},{8,9},{9,10},{10,11},{11... | collective-permute-start | bytes 294920 | tf_op jit(solution)/shard_map/ppermute | solution.py:14
  19.0 0.0 copy-done.2
  19.0 0.1 copy.46
  19.1 0.3 fusion.47
  19.6 0.0 copy-done.4
  19.6 0.1 reshape.156
  19.7 0.2 fusion.49
  19.9 2.2 %scatter_custom_fusion.1 = bf16[257]{0:T(512)(128)(2,1)S(1)} fusion(s32[256]{0:T(256)S(1)} %bitcast.73, bf16[256]{0:T(256)(128)(2,1)S(1)} %reshape.156, bf16[]{:T(256)} %constant.7.clone.1), kind=kCustom, calls=%fused_computation.61 | custom fusion | bytes 516 | tf_op jit(solution)/shard_map/scatter | solution.py:80
  22.1 0.8 reshape.163
  22.9 10.7 %all-to-all-start.1 = ((bf16[128,2,1]{1,2,0:T(2,128)(2,1)}), bf16[128,2,1]{1,2,0:T(2,128)(2,1)S(1)}, u32[]{:S(2)}, u32[]{:S(2)}) async-start(bf16[128,2,1]{1,2,0:T(2,128)(2,1)} %reshape.163), calls=%async_computation.1 | async-start | bytes 131072 | tf_op jit(solution)/shard_map/all_to_all | solution.py:84
  33.6 0.0 copy-done.5
  33.7 0.0 collective-permute-done
  33.7 0.0 collective-permute-done.1
  33.7 0.0 collective-permute-done.2
  33.7 0.0 collective-permute-done.3
  33.7 0.0 copy-done.3
  33.7 7.0 %fusion.58 = (bf16[16,16,12,128]{3,2,1,0:T(8,128)(2,1)}, f32[16,16,12,128]{3,2,1,0:T(8,128)}) fusion(f32[16,16]{1,0:T(8,128)S(1)} %broadcast_multiply_fusion, f32[16,16,12,128]{3,2,1,0:T(8,128)} %copy-done.1, f32[16,1,12,128]{3,2,1,0:T(8,128)} %collective-permute-done.3, f32[16,1,12,128]{3,2,1,0:T(8,128)} %collective-permute-done.2, ...), kind=kLoop, calls=%fused_computation.65 | loop fusion | flops 5898240 | bytes 4332544 | tf_op jit(solution)/shard_map/convert_element_type | solution.py:73
  40.7 3.4 %scatter_custom_fusion = bf16[257,1536]{1,0:T(8,128)(2,1)} fusion(s32[256]{0:T(256)S(1)} %bitcast.74, bf16[32,8,12,128]{3,2,1,0:T(8,128)(2,1)} %bitcast.66, bf16[]{:T(256)} %constant.7.clone.1), kind=kCustom, calls=%fused_computation.30 | custom fusion | bytes 1575938 | tf_op jit(solution)/shard_map/scatter | solution.py:77
  44.1 0.0 copy-start.6
  44.1 2.1 %slice.85 = bf16[256,1536]{1,0:T(8,128)(2,1)} slice(bf16[257,1536]{1,0:T(8,128)(2,1)} %scatter_custom_fusion), slice={[0:256], [0:1536]} | slice | bytes 1572864 | tf_op jit(solution)/shard_map/slice | solution.py:78
  46.2 0.0 copy-start.7
  46.2 0.0 copy-start.8
  46.2 2.9 %reshape.127 = bf16[128,2,1536]{2,1,0:T(2,128)(2,1)} reshape(bf16[256,1536]{1,0:T(8,128)(2,1)} %slice.85) | data formatting | bytes 1572864 | tf_op jit(solution)/shard_map/reshape | solution.py:78
  49.1 0.0 all-to-all-done.1
  49.1 13.7 %all-to-all-start = ((bf16[128,2,1536]{2,1,0:T(2,128)(2,1)}), bf16[128,2,1536]{2,1,0:T(2,128)(2,1)}, u32[]{:S(2)}, u32[]{:S(2)}) async-start(bf16[128,2,1536]{2,1,0:T(2,128)(2,1)} %reshape.127), calls=%async_computation | async-start | bytes 1572864 | tf_op jit(solution)/shard_map/all_to_all | solution.py:83
  62.8 0.0 copy-done.6
  62.8 0.2 convert_reduce_fusion
  63.0 0.1 reshape.132
  63.2 21.2 %all-to-all-done = bf16[128,2,1536]{2,1,0:T(2,128)(2,1)} async-done(((bf16[128,2,1536]{2,1,0:T(2,128)(2,1)}), bf16[128,2,1536]{2,1,0:T(2,128)(2,1)}, u32[]{:S(2)}, u32[]{:S(2)}) %all-to-all-start) | async-done | bytes 786464 | tf_op jit(solution)/shard_map/all_to_all | solution.py:83
  84.4 3.0 %reshape.128 = bf16[256,1536]{1,0:T(8,128)(2,1)} reshape(bf16[128,2,1536]{2,1,0:T(2,128)(2,1)} %all-to-all-done) | data formatting | bytes 1572864 | tf_op jit(solution)/shard_map/reshape | solution.py:42
  87.3 0.0 copy-done
  87.3 0.0 copy-done.7
  87.3 0.0 copy-done.8
  87.3 4.5 %multiply_convert_fusion.1 = bf16[256,1024]{1,0:T(8,128)(2,1)} fusion(bf16[1,2,1024,1024]{3,2,1,0:T(8,128)(2,1)} %param.21, bf16[256,1536]{1,0:T(8,128)(2,1)} %reshape.128, bf16[1,1536,1024]{2,1,0:T(8,128)(2,1)S(1)} %copy-done, f32[1024]{0:T(1024)S(1)} %bitcast.77, f32[1024]{0:T(1024)S(1)} %bitcast.78, f32[256]{0:T(256)S(1)} %reshape.132, f32[1024]{0:T(1024)S(1)} %bitcast.79), kind=kOutput, calls=%fused_computation.28 | convolution fusion | flops 1345847296 | bytes 6566912 | tf_op jit(solution)/shard_map/dot_general | solution.py:48
  91.8 3.0 %convolution_convert_fusion = bf16[256,512]{1,0:T(8,128)(2,1)S(1)} fusion(bf16[1,1024,512]{2,1,0:T(8,128)(2,1)} %param.23, bf16[256,1024]{1,0:T(8,128)(2,1)} %multiply_convert_fusion.1, bf16[1,2,1024,1024]{3,2,1,0:T(8,128)(2,1)} %param.21, f32[1024]{0:T(1024)S(1)} %bitcast.76), kind=kOutput, calls=%fused_computation.25 | convolution fusion | flops 807010304 | bytes 3936256 | tf_op jit(solution)/shard_map/dot_general | solution.py:52
  94.8 0.8 reshape.130
  95.6 8.9 %all-to-all-start.2 = ((bf16[128,2,512]{2,1,0:T(2,128)(2,1)}), bf16[128,2,512]{2,1,0:T(2,128)(2,1)S(1)}, u32[]{:S(2)}, u32[]{:S(2)}) async-start(bf16[128,2,512]{2,1,0:T(2,128)(2,1)} %reshape.130), calls=%async_computation.2 | async-start | bytes 524288 | tf_op jit(solution)/shard_map/all_to_all | solution.py:92
  104.6 11.9 %all-to-all-done.2 = bf16[128,2,512]{2,1,0:T(2,128)(2,1)S(1)} async-done(((bf16[128,2,512]{2,1,0:T(2,128)(2,1)}), bf16[128,2,512]{2,1,0:T(2,128)(2,1)S(1)}, u32[]{:S(2)}, u32[]{:S(2)}) %all-to-all-start.2) | async-done | bytes 262176 | tf_op jit(solution)/shard_map/all_to_all | solution.py:92
  116.5 0.8 reshape.131
  117.3 1.0 concatenate.21
  118.3 1.8 %gather_fusion = bf16[256,512]{1,0:T(8,128)(2,1)} fusion(bf16[257,512]{1,0:T(8,128)(2,1)S(1)} %concatenate.21, s32[1024]{0:T(1024)S(1)} %pad_clamp_fusion), kind=kCustom, calls=%fused_computation | custom fusion | bytes 525312 | tf_op jit(solution)/shard_map/gather | solution.py:94
  120.1 1.9 %reshape.133 = f32[16,16,4,128]{3,2,1,0:T(4,128)} reshape(bf16[256,512]{1,0:T(8,128)(2,1)} %gather_fusion) | data formatting | bytes 786432 | tf_op jit(solution)/shard_map/convert_element_type | solution.py:94
  122.0 2.3 %slice_add_fusion = f32[16,16,4,128]{3,2,1,0:T(4,128)} fusion(f32[16,16,4,128]{3,2,1,0:T(4,128)} %reshape.133, f32[16,16,12,128]{3,2,1,0:T(8,128)} %get-tuple-element.6), kind=kLoop, calls=%fused_computation.33 | loop fusion | flops 131072 | bytes 1572864 | tf_op jit(solution)/shard_map/add | solution.py:95
  (14 shorter events, 0.1 us)
Async XLA Ops:
  0.0 87.3 %copy-start = (bf16[1,1536,1024]{2,1,0:T(8,128)(2,1)S(1)}, bf16[1,1536,1024]{2,1,0:T(8,128)(2,1)}, u32[]{:S(2)}) copy-start(bf16[1,1536,1024]{2,1,0:T(8,128)(2,1)} %param.18) | copy-start | bytes 9437188
  0.0 19.0 %copy-start.2 = (s32[1,1,1,256,1]{3,4,2,1,0:T(1,128)S(1)}, s32[1,1,1,256,1]{3,4,2,1,0:T(1,128)}, u32[]{:S(2)}) copy-start(s32[1,1,1,256,1]{3,4,2,1,0:T(1,128)} %param.16) | copy-start | bytes 3076
  0.0 19.6 %copy-start.4 = (s32[16,16]{1,0:T(8,128)S(1)}, s32[16,16]{1,0:T(8,128)}, u32[]{:S(2)}) copy-start(s32[16,16]{1,0:T(8,128)} %param.15) | copy-start | bytes 3076
  0.0 33.6 %copy-start.5 = (f32[16,16]{1,0:T(8,128)S(1)}, f32[16,16]{1,0:T(8,128)}, u32[]{:S(2)}) copy-start(f32[16,16]{1,0:T(8,128)} %param.14) | copy-start | bytes 3076
  0.0 33.7 %copy-start.3 = (f32[12,128]{1,0:T(8,128)S(1)}, f32[12,128]{1,0:T(8,128)}, u32[]{:S(2)}) copy-start(f32[12,128]{1,0:T(8,128)} %param.13) | copy-start | bytes 18436
  2.1 9.6 %copy-start.1 = (f32[16,16,12,128]{3,2,1,0:T(8,128)}, f32[16,16,12,128]{3,2,1,0:T(8,128)S(1)}, u32[]{:S(2)}) copy-start(f32[16,16,12,128]{3,2,1,0:T(8,128)S(1)} %copy.45) | copy-start | bytes 4718596
  2.9 30.8 %collective-permute-start = (f32[1,16,12,128]{3,2,1,0:T(8,128)}, f32[1,16,12,128]{3,2,1,0:T(8,128)S(1)}, u32[]{:S(2)}, u32[]{:S(2)}) collective-permute-start(f32[1,16,12,128]{3,2,1,0:T(8,128)} %get-tuple-element.7), channel_id=1, source_target_pairs={{8,0},{16,8},{24,16},{32,24},{40,32},{48,40},{56,48},{64,56},{72,6... | collective-permute-start | bytes 294920 | tf_op jit(solution)/shard_map/ppermute | solution.py:17
  11.7 21.9 %collective-permute-start.1 = (f32[1,16,12,128]{3,2,1,0:T(8,128)}, f32[1,16,12,128]{3,2,1,0:T(8,128)}, u32[]{:S(2)}, u32[]{:S(2)}) collective-permute-start(f32[1,16,12,128]{3,2,1,0:T(8,128)} %get-tuple-element.8), channel_id=1, source_target_pairs={{0,8},{8,16},{16,24},{24,32},{32,40},{40,48},{48,56},{56,64},{64,7... | collective-permute-start | bytes 294920 | tf_op jit(solution)/shard_map/ppermute | solution.py:14
  12.5 21.2 %collective-permute-start.2 = (f32[16,1,12,128]{3,2,1,0:T(8,128)}, f32[16,1,12,128]{3,2,1,0:T(8,128)}, u32[]{:S(2)}, u32[]{:S(2)}) collective-permute-start(f32[16,1,12,128]{3,2,1,0:T(8,128)} %get-tuple-element.9), channel_id=1, source_target_pairs={{1,0},{2,1},{3,2},{4,3},{5,4},{6,5},{7,6},{9,8},{10,9},{11,10},{12... | collective-permute-start | bytes 294920 | tf_op jit(solution)/shard_map/ppermute | solution.py:17
  15.3 18.4 %collective-permute-start.3 = (f32[16,1,12,128]{3,2,1,0:T(8,128)}, f32[16,1,12,128]{3,2,1,0:T(8,128)}, u32[]{:S(2)}, u32[]{:S(2)}) collective-permute-start(f32[16,1,12,128]{3,2,1,0:T(8,128)} %get-tuple-element.10), channel_id=1, source_target_pairs={{0,1},{1,2},{2,3},{3,4},{4,5},{5,6},{6,7},{8,9},{9,10},{10,11},{11... | collective-permute-start | bytes 294920 | tf_op jit(solution)/shard_map/ppermute | solution.py:14
  22.9 26.2 %all-to-all-start.1 = ((bf16[128,2,1]{1,2,0:T(2,128)(2,1)}), bf16[128,2,1]{1,2,0:T(2,128)(2,1)S(1)}, u32[]{:S(2)}, u32[]{:S(2)}) async-start(bf16[128,2,1]{1,2,0:T(2,128)(2,1)} %reshape.163), calls=%async_computation.1 | async-start | bytes 131072 | tf_op jit(solution)/shard_map/all_to_all | solution.py:84
  44.1 18.7 %copy-start.6 = (f32[1,2,1024]{2,1,0:T(2,128)S(1)}, f32[1,2,1024]{2,1,0:T(2,128)}, u32[]{:S(2)}) copy-start(f32[1,2,1024]{2,1,0:T(2,128)} %param.22) | copy-start | bytes 24580
  46.2 41.1 %copy-start.7 = (f32[1,1024]{1,0:T(1,128)S(1)}, f32[1,1024]{1,0:T(1,128)}, u32[]{:S(2)}) copy-start(f32[1,1024]{1,0:T(1,128)} %param.20) | copy-start | bytes 12292
  46.2 41.1 %copy-start.8 = (f32[1,1024]{1,0:T(1,128)S(1)}, f32[1,1024]{1,0:T(1,128)}, u32[]{:S(2)}) copy-start(f32[1,1024]{1,0:T(1,128)} %param.19) | copy-start | bytes 12292
  49.1 35.3 %all-to-all-start = ((bf16[128,2,1536]{2,1,0:T(2,128)(2,1)}), bf16[128,2,1536]{2,1,0:T(2,128)(2,1)}, u32[]{:S(2)}, u32[]{:S(2)}) async-start(bf16[128,2,1536]{2,1,0:T(2,128)(2,1)} %reshape.127), calls=%async_computation | async-start | bytes 1572864 | tf_op jit(solution)/shard_map/all_to_all | solution.py:83
  95.6 20.9 %all-to-all-start.2 = ((bf16[128,2,512]{2,1,0:T(2,128)(2,1)}), bf16[128,2,512]{2,1,0:T(2,128)(2,1)S(1)}, u32[]{:S(2)}, u32[]{:S(2)}) async-start(bf16[128,2,512]{2,1,0:T(2,128)(2,1)} %reshape.130), calls=%async_computation.2 | async-start | bytes 524288 | tf_op jit(solution)/shard_map/all_to_all | solution.py:92
where the time goes:
time: 126 us; the launch traced here: 124 us
  starting transfers between devices  48.1 us (38%)
  waiting for transfers between devices  33.1 us (26%)
  local copies, waits for them, and re-layouts  24.6 us (20%)
  other arithmetic  10.1 us (8%)
  matrix products  7.5 us (6%)
    all_to_all x1, waiting for transfers between devices, body(): lax.all_to_all(outbound, ('tile', 'lat'), split_axis=0, concat_axis=0, ti...  21.2 us
    all_to_all x1, starting transfers between devices, body(): lax.all_to_all(outbound, ('tile', 'lat'), split_axis=0, concat_axis=0, ti...  13.7 us
    all_to_all x1, waiting for transfers between devices, body(): lax.all_to_all(produced, ('tile', 'lat'), split_axis=0, concat_axis=0, ti...  11.9 us
    ppermute x2, starting transfers between devices, extended(): lax.ppermute(lax.slice_in_dim(block, 0, width, axis=dim), axis, backward)  11.7 us
    all_to_all x1, starting transfers between devices, body(): lax.all_to_all(flags, ('tile', 'lat'), split_axis=0, concat_axis=0, tiled...  10.7 us
    all_to_all x1, starting transfers between devices, body(): lax.all_to_all(produced, ('tile', 'lat'), split_axis=0, concat_axis=0, ti...  8.94 us
    convert_element_type x1, other arithmetic, body(): features = advanced.astype(jnp.bfloat16).reshape(columns, fsize)  6.97 us
    dot_general x1, matrix products, run_network(): jnp.dot(hidden, w_inner[number], preferred_element_type=jnp.float32)  4.47 us
  transfers between devices with their start and end apart: 7, of which 2 were waited for; matrix products, arithmetic and copies ran while one was open for 16% of the time, Pallas kernels for 0%

commit v1 on v0

v1 whole, which is shorter than its diff:
```python
import functools

import jax
import jax.numpy as jnp
from jax import lax
from jax.experimental import pallas as pl
from jax.experimental.pallas import tpu as pltpu
from jax.sharding import PartitionSpec as P

MESH = pl.DeviceIdType.MESH
BF16 = jnp.bfloat16
F32 = jnp.float32

NY, NZ, NX = 4, 8, 4
PLANE = NY * NX
PEERS = PLANE * NZ
LON, LAT, VARS, LEV, OUTV = 16, 16, 12, 128, 4
COLS = LON * LAT
ROWS = VARS * LAT
HID = 1024
WORDS = VARS + 1


def place(step, z_off, me):
    y, z, lat = me
    d_x, d_y = lax.rem(step, NX), lax.div(step, NX)
    tile = lax.rem(y + d_y, NY) * NZ + lax.rem(z + z_off, NZ)
    return tile, lax.rem(lat + d_x, NX)


def source(step, z_off, me):
    y, z, lat = me
    d_x, d_y = lax.rem(step, NX), lax.div(step, NX)
    tile = lax.rem(y + NY - d_y, NY) * NZ + lax.rem(z + NZ - z_off, NZ)
    return tile, lax.rem(lat + NX - d_x, NX)


def slot_row(route_row, count):
    shape = (COLS, COLS)
    first = lax.broadcasted_iota(jnp.int32, shape, 0)
    second = lax.broadcasted_iota(jnp.int32, shape, 1)
    row = jnp.broadcast_to(route_row, shape)
    diagonal = jnp.where(first == second, row, 0.0)
    column = jnp.broadcast_to(jnp.sum(diagonal, axis=1, keepdims=True), shape)
    earlier = (first < second) & (row == column) & (first < count)
    rank = jnp.sum(jnp.where(earlier, 1.0, 0.0), axis=0, keepdims=True)
    position = lax.broadcasted_iota(jnp.int32, (1, COLS), 1)
    return jnp.where(position < count, 2.0 * route_row + rank, -1.0)


def slot_matrix(route_row, count):
    slots = lax.broadcasted_iota(jnp.int32, (COLS, COLS), 0).astype(F32)
    hit = slots == jnp.broadcast_to(slot_row(route_row, count), (COLS, COLS))
    return jnp.where(hit, 1.0, 0.0).astype(BF16)


def as_columns(grid, lon, width):
    shape = (LAT, LAT)
    same = lax.broadcasted_iota(jnp.int32, shape, 0) == lax.broadcasted_iota(jnp.int32, shape, 1)
    picked = jnp.where(same, jnp.broadcast_to(grid[lon : lon + 1, :], shape), 0.0)
    return jnp.broadcast_to(jnp.sum(picked, axis=1, keepdims=True), (LAT, width))


def edges_kernel(state, edges):
    edges[0] = state[pl.ds((LON - 1) * ROWS, ROWS), :].astype(BF16)
    edges[1] = state[pl.ds(0, ROWS), :].astype(BF16)
    edges[2] = state[pl.ds(LAT - 1, LON * VARS, stride=LAT), :].astype(BF16)
    edges[3] = state[pl.ds(0, LON * VARS, stride=LAT), :].astype(BF16)


def halo_kernel(edges, halos, send_sem, recv_sem):
    tile, lat, emu = lax.axis_index("tile"), lax.axis_index("lat"), lax.axis_index("emu")
    barrier = pltpu.get_barrier_semaphore()
    tiles = NZ * NY
    east = (lax.rem(tile + 1, tiles), lat, emu)
    west = (lax.rem(tile + tiles - 1, tiles), lat, emu)
    other = (tile, lat, 1 - emu)
    across = (tile, lax.rem(lat + NX - 1 + 2 * emu, NX), 1 - emu)
    for device in (east, west, other, across):
        pl.semaphore_signal(barrier, inc=1, device_id=device, device_id_type=MESH)
    pl.semaphore_wait(barrier, 4)
    copies = []
    for k, (edge, device) in enumerate(((0, east), (1, west), (2 + emu, other), (3 - emu, across))):
        copy = pltpu.make_async_remote_copy(
            src_ref=edges.at[edge], dst_ref=halos.at[edge], send_sem=send_sem.at[k],
            recv_sem=recv_sem.at[k], device_id=device, device_id_type=MESH,
        )
        copy.start()
        copies.append(copy)
    for copy in copies:
        copy.wait()


def step_kernel(state, halos, diff, wind, land, route, count, where, outbound, kept, feats):
    one_hot = slot_matrix(route[...], count[0, 0])
    sub = lax.broadcasted_iota(jnp.int32, (LAT, LEV), 0)
    winds = wind[...]
    lands = land[...].astype(F32)
    keep_south = where[0, 0].astype(F32)
    keep_north = where[0, 1].astype(F32)
    for lon in range(LON):
        gust = 0.5 * as_columns(winds, lon, LEV)
        feats[lon * LAT : (lon + 1) * LAT, VARS * LEV :] = as_columns(lands, lon, LEV).astype(BF16)
        south_rows = halos[2, lon * VARS : (lon + 1) * VARS, :].astype(F32) * keep_south
        north_rows = halos[3, lon * VARS : (lon + 1) * VARS, :].astype(F32) * keep_north
        for v in range(VARS):
            row = lon * ROWS + v * LAT
            mid = state[pl.ds(row, LAT), :]
            if lon < LON - 1:
                right = state[pl.ds(row + ROWS, LAT), :]
            else:
                right = halos[1, v * LAT : (v + 1) * LAT, :].astype(F32)
            if lon > 0:
                left = state[pl.ds(row - ROWS, LAT), :]
            else:
                left = halos[0, v * LAT : (v + 1) * LAT, :].astype(F32)
            up = jnp.where(
                sub == LAT - 1,
                jnp.broadcast_to(north_rows[v : v + 1, :], (LAT, LEV)),
                pltpu.roll(mid, LAT - 1, 0),
            )
            down = jnp.where(
                sub == 0,
                jnp.broadcast_to(south_rows[v : v + 1, :], (LAT, LEV)),
                pltpu.roll(mid, 1, 0),
            )
            spread = right + left + up + down - 4.0 * mid
            moved = mid + diff[v : v + 1, :] * spread - gust * (right - left)
            feats[lon * LAT : (lon + 1) * LAT, v * LEV : (v + 1) * LEV] = moved.astype(BF16)
            if v < OUTV:
                kept[pl.ds((lon * OUTV + v) * LAT, LAT), :] = moved
    for v in range(WORDS):
        rows = jnp.dot(one_hot, feats[:, v * LEV : (v + 1) * LEV], preferred_element_type=F32)
        outbound[v] = rows.astype(BF16).reshape(PEERS, 2, LEV)


def position():
    tile, lat, emu = lax.axis_index("tile"), lax.axis_index("lat"), lax.axis_index("emu")
    return (lax.div(tile, NZ), lax.rem(tile, NZ), lat), emu, tile * NX + lat


def greet_all(me, emu):
    barrier = pltpu.get_barrier_semaphore()

    def one(index, carry):
        tile_to, lat_to = place(lax.rem(index, PLANE), lax.div(index, PLANE), me)
        pl.semaphore_signal(
            barrier, inc=1, device_id=(tile_to, lat_to, emu), device_id_type=MESH
        )
        return carry

    lax.fori_loop(1, PEERS, one, 0)
    pl.semaphore_wait(barrier, PEERS - 1)


def z_of(index):
    half = lax.div(index + 1, 2)
    return NZ // 2 + (2 * lax.rem(index, 2) - 1) * half * (-1)


def dispatch_kernel(outbound, inbound, send_sem, recv_sem, own_sem):
    me, emu, expert = position()
    own = pltpu.make_async_copy(outbound.at[:, expert], inbound.at[:, PEERS - PLANE], own_sem)
    own.start()
    greet_all(me, emu)

    def send(index):
        step = lax.rem(index, PLANE)
        tile_to, lat_to = place(step, z_of(lax.div(index, PLANE)), me)
        return pltpu.make_async_remote_copy(
            src_ref=outbound.at[:, tile_to * NX + lat_to], dst_ref=inbound.at[:, index],
            send_sem=send_sem, recv_sem=recv_sem,
            device_id=(tile_to, lat_to, emu), device_id_type=MESH,
        )

    def start(index, carry):
        send(index).start()
        return carry

    lax.fori_loop(0, PEERS - PLANE, start, 0)
    lax.fori_loop(PEERS - PLANE + 1, PEERS, start, 0)
    pltpu.make_async_remote_copy(
        src_ref=outbound.at[:, pl.ds(0, PEERS - 1)], dst_ref=inbound.at[:, pl.ds(0, PEERS - 1)],
        send_sem=send_sem, recv_sem=recv_sem,
        device_id=(*place(1, 0, me), emu), device_id_type=MESH,
    ).wait()
    own.wait()


def return_kernel(answers, returned, send_sem, recv_sem, own_sem):
    me, emu, expert = position()
    own = pltpu.make_async_copy(answers.at[:, PEERS - PLANE], returned.at[:, expert], own_sem)
    own.start()
    greet_all(me, emu)

    def send(index):
        step = lax.rem(index, PLANE)
        tile_to, lat_to = source(step, z_of(lax.div(index, PLANE)), me)
        return pltpu.make_async_remote_copy(
            src_ref=answers.at[:, index], dst_ref=returned.at[:, expert],
            send_sem=send_sem, recv_sem=recv_sem,
            device_id=(tile_to, lat_to, emu), device_id_type=MESH,
        )

    def start(index, carry):
        send(index).start()
        return carry

    lax.fori_loop(0, PEERS - PLANE, start, 0)
    lax.fori_loop(PEERS - PLANE + 1, PEERS, start, 0)
    pltpu.make_async_remote_copy(
        src_ref=answers.at[:, pl.ds(0, PEERS - 1)], dst_ref=returned.at[:, pl.ds(0, PEERS - 1)],
        send_sem=send_sem, recv_sem=recv_sem,
        device_id=(*place(1, 0, me), emu), device_id_type=MESH,
    ).wait()
    own.wait()


def network_kernel(inbound, w_in, b_in, land_vec, w_hid, b_hid, w_out, answers):
    rows = 2 * PEERS
    taken = jnp.concatenate([inbound[v].reshape(rows, LEV) for v in range(VARS)], axis=1)
    flag = inbound[VARS].reshape(rows, LEV).astype(F32)
    flag = jnp.concatenate([flag] * (HID // LEV), axis=1)
    hidden = jnp.dot(taken, w_in[...], preferred_element_type=F32)
    hidden = jax.nn.silu(hidden + b_in[...] + flag * land_vec[...]).astype(BF16)
    for layer in range(2):
        inner = jnp.dot(hidden, w_hid[layer], preferred_element_type=F32)
        hidden = jax.nn.silu(inner + b_hid[layer : layer + 1, :]).astype(BF16)
    made = jnp.dot(hidden, w_out[...], preferred_element_type=F32).astype(BF16)
    for v in range(OUTV):
        answers[v] = made[:, v * LEV : (v + 1) * LEV].reshape(PEERS, 2, LEV)


def combine_kernel(returned, kept, route, count, out):
    one_hot = slot_matrix(route[...], count[0, 0])
    flat = jnp.concatenate([returned[v].reshape(COLS, LEV) for v in range(OUTV)], axis=1)
    tendency = lax.dot_general(
        one_hot, flat, (((0,), (0,)), ((), ())), preferred_element_type=F32
    )
    for lon in range(LON):
        for v in range(OUTV):
            base = kept[pl.ds((lon * OUTV + v) * LAT, LAT), :]
            added = tendency[lon * LAT : (lon + 1) * LAT, v * LEV : (v + 1) * LEV]
            out[pl.ds(lon * LAT * OUTV + v, LAT, stride=OUTV), :] = base + added


def body(state, diff, wind, land, routes, counts, w_in, b_in, land_vec, w_hid, b_hid, w_out):
    flat_state = jnp.transpose(state, (0, 2, 1, 3)).reshape(LON * ROWS, LEV)
    route = routes.reshape(1, COLS).astype(F32)
    count = counts.reshape(1, 1)
    lat, emu = lax.axis_index("lat"), lax.axis_index("emu")
    south = jnp.where((lat == 0) & (emu == 0), 0, 1)
    north = jnp.where((lat == NX - 1) & (emu == 1), 0, 1)
    where = jnp.stack([south, north]).reshape(1, 2).astype(jnp.int32)
    vmem = pl.BlockSpec(memory_space=pltpu.VMEM)
    smem = pl.BlockSpec(memory_space=pltpu.SMEM)
    hbm = pl.BlockSpec(memory_space=pl.ANY)
    dma = pltpu.SemaphoreType.DMA
    edge = jax.ShapeDtypeStruct((4, ROWS, LEV), BF16)
    features = jax.ShapeDtypeStruct((WORDS, PEERS, 2, LEV), BF16)
    answer = jax.ShapeDtypeStruct((OUTV, PEERS, 2, LEV), BF16)

    def remote(number):
        return pltpu.CompilerParams(
            collective_id=number, has_side_effects=True, vmem_limit_bytes=4 << 20
        )

    def local(size):
        return pltpu.CompilerParams(vmem_limit_bytes=size << 20)

    edges = pl.pallas_call(
        edges_kernel, out_shape=edge, in_specs=[vmem], out_specs=vmem,
        compiler_params=local(4), name="edges",
    )(flat_state)
    halos = pl.pallas_call(
        halo_kernel, out_shape=edge, in_specs=[hbm], out_specs=hbm,
        scratch_shapes=[dma((4,)), dma((4,))],
        compiler_params=remote(0), name="halo",
    )(edges)
    outbound, kept = pl.pallas_call(
        step_kernel,
        out_shape=(features, jax.ShapeDtypeStruct((LON * OUTV * LAT, LEV), F32)),
        in_specs=[vmem, vmem, vmem, vmem, vmem, vmem, smem, smem], out_specs=(vmem, vmem),
        scratch_shapes=[pltpu.VMEM((COLS, WORDS * LEV), BF16)],
        compiler_params=local(8), name="step",
    )(flat_state, halos, diff, wind, land, route, count, where)
    inbound = pl.pallas_call(
        dispatch_kernel, out_shape=features, in_specs=[hbm], out_specs=hbm,
        scratch_shapes=[dma, dma, dma],
        compiler_params=remote(1), name="dispatch",
    )(outbound)
    answers = pl.pallas_call(
        network_kernel, out_shape=answer,
        in_specs=[vmem] * 7, out_specs=vmem,
        compiler_params=local(24), name="network",
    )(inbound, w_in[0], b_in, land_vec, w_hid[0], b_hid[0], w_out[0])
    returned = pl.pallas_call(
        return_kernel, out_shape=answer, in_specs=[hbm], out_specs=hbm,
        scratch_shapes=[dma, dma, dma],
        compiler_params=remote(2), name="give_back",
    )(answers)
    out = pl.pallas_call(
        combine_kernel,
        out_shape=jax.ShapeDtypeStruct((COLS * OUTV, LEV), F32),
        in_specs=[vmem, vmem, vmem, smem],
        out_specs=vmem,
        compiler_params=local(8), name="combine",
    )(returned, kept, route, count)
    return out.reshape(LON, LAT, OUTV, LEV)


def solution(mesh):
    in_specs = (
        P("tile", ("lat", "emu"), None, None),
        P(),
        P("tile", ("lat", "emu")),
        P("tile", ("lat", "emu")),
        P("tile", "lat", "emu", None, None),
        P("tile", "lat", "emu"),
        P(("tile", "lat"), None, None),
        P(("tile", "lat"), None),
        P(("tile", "lat"), None),
        P(("tile", "lat"), None, None, None),
        P(("tile", "lat"), None, None),
        P(("tile", "lat"), None, None),
    )
    out_specs = P("tile", ("lat", "emu"), None, None)
    return jax.shard_map(body, mesh=mesh, in_specs=in_specs, out_specs=out_specs, check_vma=False)
```

time: 126 us -> 75.6 us (0.60); the launches traced: 124 us -> 75.3 us
  Pallas kernels: 0 us -> 66.8 us
  starting transfers between devices: 48.1 us -> 0 us
  waiting for transfers between devices: 33.1 us -> 0 us
  local copies, waits for them, and re-layouts: 24.6 us -> 6.92 us
  other arithmetic: 10.1 us -> 0.76 us
  matrix products: 7.5 us -> 0 us
    pallas_call x0 -> x7, Pallas kernels: none -> 66.8 us  [the longest x1 29.3 us: body(): pl.pallas_call(dispatch_kernel, out_shape=features, in_specs=[hbm], out_s...]
    all_to_all x3 -> x0, starting transfers between devices: 33.4 us -> none  [the longest x1 13.7 us: body(): lax.all_to_all(outbound, ('tile', 'lat'), split_axis=0, concat_axis=0, ti...]
    all_to_all x3 -> x0, waiting for transfers between devices: 33.1 us -> none  [the longest x1 21.2 us: body(): lax.all_to_all(outbound, ('tile', 'lat'), split_axis=0, concat_axis=0, ti...]
    ppermute x4 -> x0, starting transfers between devices: 14.7 us -> none  [the longest x2 11.7 us: extended(): lax.ppermute(lax.slice_in_dim(block, 0, width, axis=dim), axis, backward)]
    reshape x5 -> x0, local copies, waits for them, and re-layouts: 8.24 us -> none  [the longest x1 2.96 us: run_network(): rows = features.reshape(-1, features.shape[-1])]
    dot_general x2 -> x0, matrix products: 7.5 us -> none  [the longest x1 4.47 us: run_network(): jnp.dot(hidden, w_inner[number], preferred_element_type=jnp.float32)]
    convert_element_type x3 -> x1, other arithmetic: 7.16 us -> 0.68 us  [body(): route = routes.reshape(1, COLS).astype(F32)]
    scatter x2 -> x0, local copies, waits for them, and re-layouts: 5.6 us -> none  [the longest x1 3.44 us: body(): jnp.zeros((experts * capacity + 1, fsize), jnp.bfloat16).at[slot_index]]
  transfers between devices with their start and end apart: 7 -> 0, of which waited for: 2 -> 0; matrix products, arithmetic and copies ran while one was open for 16% -> 0% of each run, Pallas kernels for 0% -> 0%
where the time goes in v1:
time: 75.6 us; the launch traced here: 75.3 us
  Pallas kernels  66.8 us (88%)
  local copies, waits for them, and re-layouts  6.92 us (9%)
  between operations  0.8 us (1%)
  other arithmetic  0.76 us (1%)
    pallas_call x1, Pallas kernels, body(): pl.pallas_call(dispatch_kernel, out_shape=features, in_specs=[hbm], out_s...  29.3 us
    pallas_call x1, Pallas kernels, body(): pl.pallas_call(return_kernel, out_shape=answer, in_specs=[hbm], out_specs...  17.8 us
    pallas_call x1, Pallas kernels, body(): pl.pallas_call(halo_kernel, out_shape=edge, in_specs=[hbm], out_specs=hbm...  13.2 us
    unnamed x22, local copies, waits for them, and re-layouts  6.92 us
    pallas_call x1, Pallas kernels, body(): pl.pallas_call(step_kernel, out_shape=(features, jax.ShapeDtypeStruct((LO...  2.57 us
    pallas_call x1, Pallas kernels, body(): pl.pallas_call(network_kernel, out_shape=answer, in_specs=[vmem] * 7, out...  2.56 us

profile of v1, /device:TPU:1, one launch (start us, length us, event | category | flops | bytes accessed | tf_op | source)
XLA Modules:
  0.0 75.3 jit_solution(3416963221718265524)
XLA Ops:
  0.0 0.0 copy-start.8
  0.0 0.0 copy-start.10
  0.0 0.0 copy-start.9
  0.7 0.1 add_bitcast_fusion.where
  0.8 0.7 convert_bitcast_fusion.route
  1.5 0.0 copy-start
  1.5 1.4 %copy-done = f32[16,16,12,128]{3,1,2,0:T(8,128)S(1)} copy-done((f32[16,16,12,128]{3,1,2,0:T(8,128)S(1)}, f32[16,16,12,128]{3,1,2,0:T(8,128)}, u32[]{:S(2)}) %copy-start) | copy-done | bytes 1572888
  2.9 0.0 copy-start.1
  2.9 0.0 copy-start.3
  2.9 0.1 edges.1
  3.0 13.2 %halo.1.halos = bf16[4,192,128]{2,1,0:T(8,128)(2,1)S(1)} custom-call(bf16[4,192,128]{2,1,0:T(8,128)(2,1)S(1)} %edges.1), custom_call_target="tpu_custom_call" | custom-call | tf_op jit(solution)/shard_map/halo/pallas_call | solution.py:275
  16.2 0.0 copy-done.1
  16.2 0.0 copy-start.5
  16.2 0.7 copy-done.5
  16.9 0.0 copy-start.6
  16.9 0.7 copy-done.6
  17.6 0.0 copy-start.7
  17.6 0.7 copy-done.7
  18.3 2.6 %step.1 = (bf16[13,128,2,128]{3,2,1,0:T(2,128)(2,1)S(1)}, f32[1024,128]{1,0:T(8,128)S(1)}) custom-call(f32[3072,128]{1,0:T(8,128)S(1)} %bitcast.18, bf16[4,192,128]{2,1,0:T(8,128)(2,1)S(1)} %halo.1.halos, f32[12,128]{1,0:T(8,128)S(1)} %copy-done.5, f32[16,16]{1,0:T(8,128)S(1)} %copy-done.6, s32[16,16]{1,0:T(8,128)S(1)} %copy-done.7, ...), custom_call_target="tpu_custom_call" | custom-call | tf_op jit(solution)/shard_map/step/pallas_call | solution.py:280
  20.9 29.3 %dispatch.1.inbound = bf16[13,128,2,128]{3,2,1,0:T(2,128)(2,1)S(1)} custom-call(bf16[13,128,2,128]{3,2,1,0:T(2,128)(2,1)S(1)} %get-tuple-element.7.outbound), custom_call_target="tpu_custom_call" | custom-call | tf_op jit(solution)/shard_map/dispatch/pallas_call | solution.py:287
  50.2 0.0 copy-done.8
  50.2 0.0 copy-done.10
  50.2 0.0 copy-done.9
  50.2 0.0 copy-done.3
  50.2 0.0 copy-start.2
  50.2 2.2 %copy-done.2 = bf16[1,2,1024,1024]{3,2,1,0:T(8,128)(2,1)S(1)} copy-done((bf16[1,2,1024,1024]{3,2,1,0:T(8,128)(2,1)S(1)}, bf16[1,2,1024,1024]{3,2,1,0:T(8,128)(2,1)}, u32[]{:S(2)}) %copy-start.2) | copy-done | bytes 4194328
  52.4 0.0 copy-start.4
  52.4 1.2 %copy-done.4 = bf16[1,1024,512]{2,1,0:T(8,128)(2,1)S(1)} copy-done((bf16[1,1024,512]{2,1,0:T(8,128)(2,1)S(1)}, bf16[1,1024,512]{2,1,0:T(8,128)(2,1)}, u32[]{:S(2)}) %copy-start.4) | copy-done | bytes 1048600
  53.6 2.6 %network.1.answers = bf16[4,128,2,128]{3,2,1,0:T(2,128)(2,1)S(1)} custom-call(bf16[13,128,2,128]{3,2,1,0:T(2,128)(2,1)S(1)} %dispatch.1.inbound, bf16[1536,1024]{1,0:T(8,128)(2,1)S(1)} %bitcast.20, f32[1,1024]{1,0:T(1,128)S(1)} %copy-done.9, f32[1,1024]{1,0:T(1,128)S(1)} %copy-done.10, bf16[2,1024,1024]{2,1,0:T(8,128)(2,1)S(1)} %bitcast.19, ...), custom_call_target="tpu_custom_call" | custom-call | tf_op jit(solution)/shard_map/network/pallas_call | solution.py:292
  56.2 17.8 %give_back.1.returned = bf16[4,128,2,128]{3,2,1,0:T(2,128)(2,1)S(1)} custom-call(bf16[4,128,2,128]{3,2,1,0:T(2,128)(2,1)S(1)} %network.1.answers), custom_call_target="tpu_custom_call" | custom-call | tf_op jit(solution)/shard_map/give_back/pallas_call | solution.py:297
  74.0 1.2 %combine.1 = f32[1024,128]{1,0:T(8,128)} custom-call(bf16[4,128,2,128]{3,2,1,0:T(2,128)(2,1)S(1)} %give_back.1.returned, f32[1024,128]{1,0:T(8,128)S(1)} %get-tuple-element.8.kept, f32[1,256]{1,0:T(1,128)S(1)} %convert_bitcast_fusion.route, s32[1,1]{1,0:T(1,128)} %bitcast.16.count), custom_call_target="tpu_custom_call" | custom-call | tf_op jit(solution)/shard_map/combine/pallas_call | solution.py:302
Async XLA Ops:
  0.0 50.2 %copy-start.8 = (f32[1,2,1024]{2,1,0:T(2,128)S(1)}, f32[1,2,1024]{2,1,0:T(2,128)}, u32[]{:S(2)}) copy-start(f32[1,2,1024]{2,1,0:T(2,128)} %param.22) | copy-start | bytes 24580
  0.0 50.2 %copy-start.10 = (f32[1,1024]{1,0:T(1,128)S(1)}, f32[1,1024]{1,0:T(1,128)}, u32[]{:S(2)}) copy-start(f32[1,1024]{1,0:T(1,128)} %land_vec.1) | copy-start | bytes 12292
  0.0 50.2 %copy-start.9 = (f32[1,1024]{1,0:T(1,128)S(1)}, f32[1,1024]{1,0:T(1,128)}, u32[]{:S(2)}) copy-start(f32[1,1024]{1,0:T(1,128)} %b_in.1) | copy-start | bytes 12292
  1.5 1.4 %copy-start = (f32[16,16,12,128]{3,1,2,0:T(8,128)S(1)}, f32[16,16,12,128]{3,1,2,0:T(8,128)}, u32[]{:S(2)}) copy-start(f32[16,16,12,128]{3,1,2,0:T(8,128)} %param.12) | copy-start | bytes 4718596
  2.9 13.3 %copy-start.1 = (f32[16,16,12,128]{3,1,2,0:T(8,128)S(1)}, f32[16,16,12,128]{3,1,2,0:T(8,128)}, u32[]{:S(2)}) copy-start(f32[16,16,12,128]{3,1,2,0:T(8,128)} %param.12) | copy-start | bytes 4718596
  2.9 47.3 %copy-start.3 = (bf16[1,1536,1024]{2,1,0:T(8,128)(2,1)S(1)}, bf16[1,1536,1024]{2,1,0:T(8,128)(2,1)}, u32[]{:S(2)}) copy-start(bf16[1,1536,1024]{2,1,0:T(8,128)(2,1)} %param.18) | copy-start | bytes 9437188
  16.2 0.7 copy-start.5
  16.9 0.7 copy-start.6
  17.6 0.7 copy-start.7
  50.2 2.2 %copy-start.2 = (bf16[1,2,1024,1024]{3,2,1,0:T(8,128)(2,1)S(1)}, bf16[1,2,1024,1024]{3,2,1,0:T(8,128)(2,1)}, u32[]{:S(2)}) copy-start(bf16[1,2,1024,1024]{3,2,1,0:T(8,128)(2,1)} %param.21) | copy-start | bytes 12582916
  52.4 1.2 %copy-start.4 = (bf16[1,1024,512]{2,1,0:T(8,128)(2,1)S(1)}, bf16[1,1024,512]{2,1,0:T(8,128)(2,1)}, u32[]{:S(2)}) copy-start(bf16[1,1024,512]{2,1,0:T(8,128)(2,1)} %param.23) | copy-start | bytes 3145732

commit v2 on v1

--- a/solution.py
+++ b/solution.py
@@ -19,6 +19,9 @@
 ROWS = VARS * LAT
 HID = 1024
 WORDS = VARS + 1
+
+
+PIECES = ((0, 80), (80, 128))
 
 
 def place(step, z_off, me):
@@ -61,11 +64,24 @@
     return jnp.broadcast_to(jnp.sum(picked, axis=1, keepdims=True), (LAT, width))
 
 
-def edges_kernel(state, edges):
-    edges[0] = state[pl.ds((LON - 1) * ROWS, ROWS), :].astype(BF16)
-    edges[1] = state[pl.ds(0, ROWS), :].astype(BF16)
-    edges[2] = state[pl.ds(LAT - 1, LON * VARS, stride=LAT), :].astype(BF16)
-    edges[3] = state[pl.ds(0, LON * VARS, stride=LAT), :].astype(BF16)
+def prepare_kernel(
+    state, diff, wind, land, route,
+    edges, state_out, diff_out, wind_out, land_out, route_out, sems,
+):
+    copies = [
+        pltpu.make_async_copy(source, target, sems.at[k])
+        for k, (source, target) in enumerate(
+            ((state, state_out), (diff, diff_out), (wind, wind_out), (land, land_out), (route, route_out))
+        )
+    ]
+    for copy in copies:
+        copy.start()
+    for copy in copies:
+        copy.wait()
+    edges[0] = state_out[pl.ds((LON - 1) * ROWS, ROWS), :].astype(BF16)
+    edges[1] = state_out[pl.ds(0, ROWS), :].astype(BF16)
+    edges[2] = state_out[pl.ds(LAT - 1, LON * VARS, stride=LAT), :].astype(BF16)
+    edges[3] = state_out[pl.ds(0, LON * VARS, stride=LAT), :].astype(BF16)
 
 
 def halo_kernel(edges, halos, send_sem, recv_sem):
@@ -91,13 +107,14 @@
         copy.wait()
 
 
-def step_kernel(state, halos, diff, wind, land, route, count, where, outbound, kept, feats):
-    one_hot = slot_matrix(route[...], count[0, 0])
+def step_kernel(state, halos, diff, wind, land, route, count, outbound, kept, feats):
+    one_hot = slot_matrix(route[...].astype(F32), count[0, 0])
     sub = lax.broadcasted_iota(jnp.int32, (LAT, LEV), 0)
     winds = wind[...]
     lands = land[...].astype(F32)
-    keep_south = where[0, 0].astype(F32)
-    keep_north = where[0, 1].astype(F32)
+    lat, emu = lax.axis_index("lat"), lax.axis_index("emu")
+    keep_south = jnp.where((lat == 0) & (emu == 0), 0.0, 1.0).astype(F32)
+    keep_north = jnp.where((lat == NX - 1) & (emu == 1), 0.0, 1.0).astype(F32)
     for lon in range(LON):
         gust = 0.5 * as_columns(winds, lon, LEV)
         feats[lon * LAT : (lon + 1) * LAT, VARS * LEV :] = as_columns(lands, lon, LEV).astype(BF16)
@@ -158,81 +175,86 @@
     return NZ // 2 + (2 * lax.rem(index, 2) - 1) * half * (-1)
 
 
-def dispatch_kernel(outbound, inbound, send_sem, recv_sem, own_sem):
-    me, emu, expert = position()
-    own = pltpu.make_async_copy(outbound.at[:, expert], inbound.at[:, PEERS - PLANE], own_sem)
-    own.start()
-    greet_all(me, emu)
-
-    def send(index):
-        step = lax.rem(index, PLANE)
-        tile_to, lat_to = place(step, z_of(lax.div(index, PLANE)), me)
-        return pltpu.make_async_remote_copy(
-            src_ref=outbound.at[:, tile_to * NX + lat_to], dst_ref=inbound.at[:, index],
-            send_sem=send_sem, recv_sem=recv_sem,
-            device_id=(tile_to, lat_to, emu), device_id_type=MESH,
-        )
-
-    def start(index, carry):
-        send(index).start()
-        return carry
-
-    lax.fori_loop(0, PEERS - PLANE, start, 0)
-    lax.fori_loop(PEERS - PLANE + 1, PEERS, start, 0)
-    pltpu.make_async_remote_copy(
-        src_ref=outbound.at[:, pl.ds(0, PEERS - 1)], dst_ref=inbound.at[:, pl.ds(0, PEERS - 1)],
-        send_sem=send_sem, recv_sem=recv_sem,
-        device_id=(*place(1, 0, me), emu), device_id_type=MESH,
-    ).wait()
-    own.wait()
-
-
-def return_kernel(answers, returned, send_sem, recv_sem, own_sem):
-    me, emu, expert = position()
-    own = pltpu.make_async_copy(answers.at[:, PEERS - PLANE], returned.at[:, expert], own_sem)
-    own.start()
-    greet_all(me, emu)
-
-    def send(index):
-        step = lax.rem(index, PLANE)
-        tile_to, lat_to = source(step, z_of(lax.div(index, PLANE)), me)
-        return pltpu.make_async_remote_copy(
-            src_ref=answers.at[:, index], dst_ref=returned.at[:, expert],
-            send_sem=send_sem, recv_sem=recv_sem,
-            device_id=(tile_to, lat_to, emu), device_id_type=MESH,
-        )
-
-    def start(index, carry):
-        send(index).start()
-        return carry
-
-    lax.fori_loop(0, PEERS - PLANE, start, 0)
-    lax.fori_loop(PEERS - PLANE + 1, PEERS, start, 0)
-    pltpu.make_async_remote_copy(
-        src_ref=answers.at[:, pl.ds(0, PEERS - 1)], dst_ref=returned.at[:, pl.ds(0, PEERS - 1)],
-        send_sem=send_sem, recv_sem=recv_sem,
-        device_id=(*place(1, 0, me), emu), device_id_type=MESH,
-    ).wait()
-    own.wait()
-
-
-def network_kernel(inbound, w_in, b_in, land_vec, w_hid, b_hid, w_out, answers):
-    rows = 2 * PEERS
-    taken = jnp.concatenate([inbound[v].reshape(rows, LEV) for v in range(VARS)], axis=1)
-    flag = inbound[VARS].reshape(rows, LEV).astype(F32)
+def network(inbound, span, rows, w_in, b_in, land_vec, w_hid, b_hid, w_out):
+    taken = jnp.concatenate([inbound[v, span].reshape(rows, LEV) for v in range(VARS)], axis=1)
+    flag = inbound[VARS, span].reshape(rows, LEV).astype(F32)
     flag = jnp.concatenate([flag] * (HID // LEV), axis=1)
     hidden = jnp.dot(taken, w_in[...], preferred_element_type=F32)
     hidden = jax.nn.silu(hidden + b_in[...] + flag * land_vec[...]).astype(BF16)
     for layer in range(2):
         inner = jnp.dot(hidden, w_hid[layer], preferred_element_type=F32)
         hidden = jax.nn.silu(inner + b_hid[layer : layer + 1, :]).astype(BF16)
-    made = jnp.dot(hidden, w_out[...], preferred_element_type=F32).astype(BF16)
-    for v in range(OUTV):
-        answers[v] = made[:, v * LEV : (v + 1) * LEV].reshape(PEERS, 2, LEV)
+    return jnp.dot(hidden, w_out[...], preferred_element_type=F32).astype(BF16)
+
+
+def exchange_kernel(
+    outbound, w_in, b_in, land_vec, w_hid, b_hid, w_out, returned,
+    inbound, answers, go_send, go_recv, back_send, back_recv, own_sem,
+):
+    me, emu, expert = position()
+    own_slot = PEERS - PLANE
+    own = pltpu.make_async_copy(outbound.at[:, expert], inbound.at[:, own_slot], own_sem.at[0])
+    own.start()
+    greet_all(me, emu)
+
+    def forward(piece, index):
+        tile_to, lat_to = place(lax.rem(index, PLANE), z_of(lax.div(index, PLANE)), me)
+        return pltpu.make_async_remote_copy(
+            src_ref=outbound.at[:, tile_to * NX + lat_to], dst_ref=inbound.at[:, index],
+            send_sem=go_send.at[piece], recv_sem=go_recv.at[piece],
+            device_id=(tile_to, lat_to, emu), device_id_type=MESH,
+        )
+
+    def backward(piece, index):
+        tile_to, lat_to = source(lax.rem(index, PLANE), z_of(lax.div(index, PLANE)), me)
+        return pltpu.make_async_remote_copy(
+            src_ref=answers.at[:, index], dst_ref=returned.at[:, expert],
+            send_sem=back_send.at[piece], recv_sem=back_recv.at[piece],
+            device_id=(tile_to, lat_to, emu), device_id_type=MESH,
+        )
+
+    def start_all(make, piece, first, last):
+        def one(index, carry):
+            make(piece, index).start()
+            return carry
+
+        if first <= own_slot < last:
+            lax.fori_loop(first, own_slot, one, 0)
+            lax.fori_loop(own_slot + 1, last, one, 0)
+        else:
+            lax.fori_loop(first, last, one, 0)
+
+    def finish(source_ref, target_ref, send_sem, recv_sem, piece, first, last):
+        size = last - first - (1 if first <= own_slot < last else 0)
+        pltpu.make_async_remote_copy(
+            src_ref=source_ref.at[:, pl.ds(0, size)], dst_ref=target_ref.at[:, pl.ds(0, size)],
+            send_sem=send_sem.at[piece], recv_sem=recv_sem.at[piece],
+            device_id=(*place(1, 0, me), emu), device_id_type=MESH,
+        ).wait()
+
+    for piece, (first, last) in enumerate(PIECES):
+        start_all(forward, piece, first, last)
+    for piece, (first, last) in enumerate(PIECES):
+        finish(outbound, inbound, go_send, go_recv, piece, first, last)
+        if first <= own_slot < last:
+            own.wait()
+        span = slice(first, last)
+        made = network(
+            inbound, span, 2 * (last - first), w_in, b_in, land_vec, w_hid, b_hid, w_out
+        )
+        for v in range(OUTV):
+            part = made[:, v * LEV : (v + 1) * LEV]
+            answers[v, span] = part.reshape(last - first, 2, LEV)
+        start_all(backward, piece, first, last)
+    mine = pltpu.make_async_copy(answers.at[:, own_slot], returned.at[:, expert], own_sem.at[1])
+    mine.start()
+    for piece, (first, last) in enumerate(PIECES):
+        finish(answers, returned, back_send, back_recv, piece, first, last)
+    mine.wait()
 
 
 def combine_kernel(returned, kept, route, count, out):
-    one_hot = slot_matrix(route[...], count[0, 0])
+    one_hot = slot_matrix(route[...].astype(F32), count[0, 0])
     flat = jnp.concatenate([returned[v].reshape(COLS, LEV) for v in range(OUTV)], axis=1)
     tendency = lax.dot_general(
         one_hot, flat, (((0,), (0,)), ((), ())), preferred_element_type=F32
@@ -246,59 +268,57 @@
 
 def body(state, diff, wind, land, routes, counts, w_in, b_in, land_vec, w_hid, b_hid, w_out):
     flat_state = jnp.transpose(state, (0, 2, 1, 3)).reshape(LON * ROWS, LEV)
-    route = routes.reshape(1, COLS).astype(F32)
+    route = routes.reshape(1, COLS)
     count = counts.reshape(1, 1)
-    lat, emu = lax.axis_index("lat"), lax.axis_index("emu")
-    south = jnp.where((lat == 0) & (emu == 0), 0, 1)
-    north = jnp.where((lat == NX - 1) & (emu == 1), 0, 1)
-    where = jnp.stack([south, north]).reshape(1, 2).astype(jnp.int32)
     vmem = pl.BlockSpec(memory_space=pltpu.VMEM)
     smem = pl.BlockSpec(memory_space=pltpu.SMEM)
-    hbm = pl.BlockSpec(memory_space=pl.ANY)
+    hbm = pl.BlockSpec(memory_space=pltpu.HBM)
+    anywhere = pl.BlockSpec(memory_space=pl.ANY)
     dma = pltpu.SemaphoreType.DMA
     edge = jax.ShapeDtypeStruct((4, ROWS, LEV), BF16)
     features = jax.ShapeDtypeStruct((WORDS, PEERS, 2, LEV), BF16)
     answer = jax.ShapeDtypeStruct((OUTV, PEERS, 2, LEV), BF16)
-
-    def remote(number):
+    loaded = [jax.ShapeDtypeStruct(x.shape, x.dtype) for x in (flat_state, diff, wind, land, route)]
+
+    def remote(number, size):
         return pltpu.CompilerParams(
-            collective_id=number, has_side_effects=True, vmem_limit_bytes=4 << 20
+            collective_id=number, has_side_effects=True, vmem_limit_bytes=size << 20
         )
 
     def local(size):
         return pltpu.CompilerParams(vmem_limit_bytes=size << 20)
 
-    edges = pl.pallas_call(
-        edges_kernel, out_shape=edge, in_specs=[vmem], out_specs=vmem,
-        compiler_params=local(4), name="edges",
-    )(flat_state)
+    def cost(flops, size):
+        return pl.CostEstimate(flops=flops, bytes_accessed=size, transcendentals=0)
+
+    edges, flat_state, diff, wind, land, route = pl.pallas_call(
+        prepare_kernel, out_shape=[edge] + loaded, in_specs=[hbm] * 5, out_specs=[vmem] * 6,
+        scratch_shapes=[dma((5,))], cost_estimate=cost(10**7, 2 * 10**6),
+        compiler_params=local(4), name="prepare",
+    )(*[pltpu.with_memory_space_constraint(x, pltpu.HBM) for x in (flat_state, diff, wind, land, route)])
     halos = pl.pallas_call(
-        halo_kernel, out_shape=edge, in_specs=[hbm], out_specs=hbm,
-        scratch_shapes=[dma((4,)), dma((4,))],
-        compiler_params=remote(0), name="halo",
+        halo_kernel, out_shape=edge, in_specs=[anywhere], out_specs=anywhere,
+        scratch_shapes=[dma((4,)), dma((4,))], cost_estimate=cost(10**10, 2 * 10**7),
+        compiler_params=remote(0, 4), name="halo",
     )(edges)
     outbound, kept = pl.pallas_call(
         step_kernel,
         out_shape=(features, jax.ShapeDtypeStruct((LON * OUTV * LAT, LEV), F32)),
-        in_specs=[vmem, vmem, vmem, vmem, vmem, vmem, smem, smem], out_specs=(vmem, vmem),
-        scratch_shapes=[pltpu.VMEM((COLS, WORDS * LEV), BF16)],
+        in_specs=[vmem, vmem, vmem, vmem, vmem, vmem, smem], out_specs=(vmem, vmem),
+        scratch_shapes=[pltpu.VMEM((COLS, WORDS * LEV), BF16)], cost_estimate=cost(10**10, 2 * 10**7),
         compiler_params=local(8), name="step",
-    )(flat_state, halos, diff, wind, land, route, count, where)
-    inbound = pl.pallas_call(
-        dispatch_kernel, out_shape=features, in_specs=[hbm], out_specs=hbm,
-        scratch_shapes=[dma, dma, dma],
-        compiler_params=remote(1), name="dispatch",
-    )(outbound)
-    answers = pl.pallas_call(
-        network_kernel, out_shape=answer,
-        in_specs=[vmem] * 7, out_specs=vmem,
-        compiler_params=local(24), name="network",
-    )(inbound, w_in[0], b_in, land_vec, w_hid[0], b_hid[0], w_out[0])
+    )(flat_state, halos, diff, wind, land, route, count)
     returned = pl.pallas_call(
-        return_kernel, out_shape=answer, in_specs=[hbm], out_specs=hbm,
-        scratch_shapes=[dma, dma, dma],
-        compiler_params=remote(2), name="give_back",
-    )(answers)
+        exchange_kernel, out_shape=answer,
+        in_specs=[anywhere] + [vmem] * 6, out_specs=anywhere,
+        scratch_shapes=[
+            pltpu.VMEM(features.shape, BF16),
+            pltpu.VMEM(answer.shape, BF16),
+            dma((2,)), dma((2,)), dma((2,)), dma((2,)), dma((2,)),
+        ],
+        cost_estimate=cost(2 * 10**9, 10**7),
+        compiler_params=remote(1, 20), name="exchange",
+    )(outbound, w_in[0], b_in, land_vec, w_hid[0], b_hid[0], w_out[0])
     out = pl.pallas_call(
         combine_kernel,
         out_shape=jax.ShapeDtypeStruct((COLS * OUTV, LEV), F32),

time: 75.6 us -> 59.7 us (0.79)
  Pallas kernels: 66.8 us -> 57.5 us
  local copies, waits for them, and re-layouts: 6.92 us -> 1.31 us
  other arithmetic: 0.76 us -> 0 us
    pallas_call x5 -> x3, Pallas kernels: 63 us -> 54.2 us  [the longest x1 39.5 us: body(): pl.pallas_call(exchange_kernel, out_shape=answer, in_specs=[anywhere] + [...]
    unnamed x22 -> x12, local copies, waits for them, and re-layouts: 6.92 us -> 1.31 us
where the time goes in v2:
time: 59.7 us; the launch traced here: 59.6 us
  Pallas kernels  57.5 us (96%)
  local copies, waits for them, and re-layouts  1.31 us (2%)
  between operations  0.73 us (1%)
    pallas_call x1, Pallas kernels, body(): pl.pallas_call(exchange_kernel, out_shape=answer, in_specs=[anywhere] + [...  39.5 us
    pallas_call x1, Pallas kernels, body(): pl.pallas_call(halo_kernel, out_shape=edge, in_specs=[anywhere], out_spec...  13.2 us
    pallas_call x1, Pallas kernels, body(): pl.pallas_call(step_kernel, out_shape=(features, jax.ShapeDtypeStruct((LO...  2.02 us
    pallas_call x1, Pallas kernels, body(): pl.pallas_call(prepare_kernel, out_shape=[edge] + loaded, in_specs=[hbm]...  1.56 us
    unnamed x12, local copies, waits for them, and re-layouts  1.31 us
    pallas_call x1, Pallas kernels, body(): pl.pallas_call(combine_kernel, out_shape=jax.ShapeDtypeStruct((COLS * OUT...  1.25 us

profile of v2, /device:TPU:1, one launch (start us, length us, event | category | flops | bytes accessed | tf_op | source)
XLA Modules:
  0.0 59.6 jit_solution(13010246945061253490)
XLA Ops:
  0.7 1.6 %prepare.1 = (bf16[4,192,128]{2,1,0:T(8,128)(2,1)S(1)}, f32[3072,128]{1,0:T(8,128)S(1)}, f32[12,128]{1,0:T(8,128)S(1)}, f32[16,16]{1,0:T(8,128)S(1)}, s32[16,16]{1,0:T(8,128)S(1)}, /*index=5*/s32[1,256]{1,0:T(1,128)S(1)}) custom-call(f32[3072,128]{1,0:T(8,128)} %bitcast.16, f32[12,128]{1,0:T(8,128)} %diff.1, f32[16,16]{1,0:T(8,128)} %wind.1, s32[16,16]{1,0:T(8,128)} %land.1, ...), custom_call_target="tpu_custom_call" | custom-call | flops 10000000 | bytes 2000000 | tf_op jit(solution)/shard_map/prepare/pallas_call | solution.py:294
  2.2 13.2 %halo.1.halos = bf16[4,192,128]{2,1,0:T(8,128)(2,1)S(1)} custom-call(bf16[4,192,128]{2,1,0:T(8,128)(2,1)S(1)} %get-tuple-element.14.edges), custom_call_target="tpu_custom_call" | custom-call | flops 10000000000 | bytes 20000000 | tf_op jit(solution)/shard_map/halo/pallas_call | solution.py:299
  15.4 0.0 copy-start
  15.4 0.0 copy-start.1
  15.4 0.0 copy-start.2
  15.5 0.0 copy-start.3
  15.5 0.0 copy-start.4
  15.5 0.0 copy-start.5
  15.5 2.0 %step.1 = (bf16[13,128,2,128]{3,2,1,0:T(2,128)(2,1)S(1)}, f32[1024,128]{1,0:T(8,128)S(1)}) custom-call(f32[3072,128]{1,0:T(8,128)S(1)} %get-tuple-element.13.state, bf16[4,192,128]{2,1,0:T(8,128)(2,1)S(1)} %halo.1.halos, f32[12,128]{1,0:T(8,128)S(1)} %get-tuple-element.15.diff, f32[16,16]{1,0:T(8,128)S(1)} %get-tuple-element.16.wind, ...), custom_call_target="tpu_custom_call" | custom-call | flops 10000000000 | bytes 20000000 | tf_op jit(solution)/shard_map/step/pallas_call | solution.py:304
  17.5 0.1 copy-done
  17.6 1.0 %copy-done.1 = bf16[1,1536,1024]{2,1,0:T(8,128)(2,1)S(1)} copy-done((bf16[1,1536,1024]{2,1,0:T(8,128)(2,1)S(1)}, bf16[1,1536,1024]{2,1,0:T(8,128)(2,1)}, u32[]{:S(2)}) %copy-start.1) | copy-done | bytes 3145752
  18.6 0.2 copy-done.2
  18.8 0.0 copy-done.3
  18.8 0.0 copy-done.4
  18.8 0.0 copy-done.5
  18.8 39.5 %exchange.1.returned = bf16[4,128,2,128]{3,2,1,0:T(2,128)(2,1)S(1)} custom-call(bf16[13,128,2,128]{3,2,1,0:T(2,128)(2,1)S(1)} %get-tuple-element.19.outbound, bf16[1536,1024]{1,0:T(8,128)(2,1)S(1)} %bitcast.13, f32[1,1024]{1,0:T(1,128)S(1)} %copy-done.4, f32[1,1024]{1,0:T(1,128)S(1)} %copy-done.5, bf16[2,1024,1024]{2,1,0:T(8,128)(2,1)S(1)} %bitcast.12, ...), custom_call_target="tpu_custom_call" | custom-call | flops 2000000000 | bytes 10000000 | tf_op jit(solution)/shard_map/exchange/pallas_call | solution.py:311
  58.3 1.3 %combine.1 = f32[1024,128]{1,0:T(8,128)} custom-call(bf16[4,128,2,128]{3,2,1,0:T(2,128)(2,1)S(1)} %exchange.1.returned, f32[1024,128]{1,0:T(8,128)S(1)} %get-tuple-element.20.kept, s32[1,256]{1,0:T(1,128)S(1)} %get-tuple-element.18.route, s32[1,1]{1,0:T(1,128)} %bitcast.11.count), custom_call_target="tpu_custom_call" | custom-call | tf_op jit(solution)/shard_map/combine/pallas_call | solution.py:322
Async XLA Ops:
  15.4 2.2 %copy-start = (bf16[1,2,1024,1024]{3,2,1,0:T(8,128)(2,1)S(1)}, bf16[1,2,1024,1024]{3,2,1,0:T(8,128)(2,1)}, u32[]{:S(2)}) copy-start(bf16[1,2,1024,1024]{3,2,1,0:T(8,128)(2,1)} %param.21) | copy-start | bytes 12582916
  15.4 3.2 %copy-start.1 = (bf16[1,1536,1024]{2,1,0:T(8,128)(2,1)S(1)}, bf16[1,1536,1024]{2,1,0:T(8,128)(2,1)}, u32[]{:S(2)}) copy-start(bf16[1,1536,1024]{2,1,0:T(8,128)(2,1)} %param.18) | copy-start | bytes 9437188
  15.4 3.4 %copy-start.2 = (bf16[1,1024,512]{2,1,0:T(8,128)(2,1)S(1)}, bf16[1,1024,512]{2,1,0:T(8,128)(2,1)}, u32[]{:S(2)}) copy-start(bf16[1,1024,512]{2,1,0:T(8,128)(2,1)} %param.23) | copy-start | bytes 3145732
  15.5 3.4 %copy-start.3 = (f32[1,2,1024]{2,1,0:T(2,128)S(1)}, f32[1,2,1024]{2,1,0:T(2,128)}, u32[]{:S(2)}) copy-start(f32[1,2,1024]{2,1,0:T(2,128)} %param.22) | copy-start | bytes 24580
  15.5 3.3 %copy-start.4 = (f32[1,1024]{1,0:T(1,128)S(1)}, f32[1,1024]{1,0:T(1,128)}, u32[]{:S(2)}) copy-start(f32[1,1024]{1,0:T(1,128)} %b_in.1) | copy-start | bytes 12292
  15.5 3.3 %copy-start.5 = (f32[1,1024]{1,0:T(1,128)S(1)}, f32[1,1024]{1,0:T(1,128)}, u32[]{:S(2)}) copy-start(f32[1,1024]{1,0:T(1,128)} %land_vec.1) | copy-start | bytes 12292

commit v3 on v2

--- a/solution.py
+++ b/solution.py
@@ -57,10 +57,10 @@
     return jnp.where(hit, 1.0, 0.0).astype(BF16)
 
 
-def as_columns(grid, lon, width):
+def as_columns(row, width):
     shape = (LAT, LAT)
     same = lax.broadcasted_iota(jnp.int32, shape, 0) == lax.broadcasted_iota(jnp.int32, shape, 1)
-    picked = jnp.where(same, jnp.broadcast_to(grid[lon : lon + 1, :], shape), 0.0)
+    picked = jnp.where(same, jnp.broadcast_to(row, shape), 0.0)
     return jnp.broadcast_to(jnp.sum(picked, axis=1, keepdims=True), (LAT, width))
 
 
@@ -107,45 +107,41 @@
         copy.wait()
 
 
-def step_kernel(state, halos, diff, wind, land, route, count, outbound, kept, feats):
+def advance(
+    state, halos, diff, wind, land, route, count, lat, emu, outbound, kept, feats, sides,
+):
     one_hot = slot_matrix(route[...].astype(F32), count[0, 0])
     sub = lax.broadcasted_iota(jnp.int32, (LAT, LEV), 0)
-    winds = wind[...]
-    lands = land[...].astype(F32)
-    lat, emu = lax.axis_index("lat"), lax.axis_index("emu")
-    keep_south = jnp.where((lat == 0) & (emu == 0), 0.0, 1.0).astype(F32)
-    keep_north = jnp.where((lat == NX - 1) & (emu == 1), 0.0, 1.0).astype(F32)
-    for lon in range(LON):
-        gust = 0.5 * as_columns(winds, lon, LEV)
-        feats[lon * LAT : (lon + 1) * LAT, VARS * LEV :] = as_columns(lands, lon, LEV).astype(BF16)
-        south_rows = halos[2, lon * VARS : (lon + 1) * VARS, :].astype(F32) * keep_south
-        north_rows = halos[3, lon * VARS : (lon + 1) * VARS, :].astype(F32) * keep_north
+    sides[0] = halos[2].astype(F32) * jnp.where((lat == 0) & (emu == 0), 0.0, 1.0).astype(F32)
+    sides[1] = halos[3].astype(F32) * jnp.where((lat == NX - 1) & (emu == 1), 0.0, 1.0).astype(F32)
+
+    def one(lon, carry):
+        gust = 0.5 * as_columns(wind[pl.ds(lon, 1), :], LEV)
+        place_of = pl.ds(pl.multiple_of(lon * LAT, LAT), LAT)
+        surface = as_columns(land[pl.ds(lon, 1), :].astype(F32), LEV)
+        feats[place_of, VARS * LEV :] = surface.astype(BF16)
+        here = lon * ROWS
+        east = jnp.minimum(lon + 1, LON - 1) * ROWS
+        west = jnp.maximum(lon - 1, 0) * ROWS
         for v in range(VARS):
-            row = lon * ROWS + v * LAT
-            mid = state[pl.ds(row, LAT), :]
-            if lon < LON - 1:
-                right = state[pl.ds(row + ROWS, LAT), :]
-            else:
-                right = halos[1, v * LAT : (v + 1) * LAT, :].astype(F32)
-            if lon > 0:
-                left = state[pl.ds(row - ROWS, LAT), :]
-            else:
-                left = halos[0, v * LAT : (v + 1) * LAT, :].astype(F32)
-            up = jnp.where(
-                sub == LAT - 1,
-                jnp.broadcast_to(north_rows[v : v + 1, :], (LAT, LEV)),
-                pltpu.roll(mid, LAT - 1, 0),
-            )
-            down = jnp.where(
-                sub == 0,
-                jnp.broadcast_to(south_rows[v : v + 1, :], (LAT, LEV)),
-                pltpu.roll(mid, 1, 0),
-            )
+            inner = slice(v * LAT, (v + 1) * LAT)
+            mid = state[pl.ds(pl.multiple_of(here + v * LAT, LAT), LAT), :]
+            right = state[pl.ds(pl.multiple_of(east + v * LAT, LAT), LAT), :]
+            left = state[pl.ds(pl.multiple_of(west + v * LAT, LAT), LAT), :]
+            right = jnp.where(lon == LON - 1, halos[1, inner, :].astype(F32), right)
+            left = jnp.where(lon == 0, halos[0, inner, :].astype(F32), left)
+            south = jnp.broadcast_to(sides[0, pl.ds(lon * VARS + v, 1), :], (LAT, LEV))
+            north = jnp.broadcast_to(sides[1, pl.ds(lon * VARS + v, 1), :], (LAT, LEV))
+            up = jnp.where(sub == LAT - 1, north, pltpu.roll(mid, LAT - 1, 0))
+            down = jnp.where(sub == 0, south, pltpu.roll(mid, 1, 0))
             spread = right + left + up + down - 4.0 * mid
             moved = mid + diff[v : v + 1, :] * spread - gust * (right - left)
-            feats[lon * LAT : (lon + 1) * LAT, v * LEV : (v + 1) * LEV] = moved.astype(BF16)
+            feats[place_of, v * LEV : (v + 1) * LEV] = moved.astype(BF16)
             if v < OUTV:
-                kept[pl.ds((lon * OUTV + v) * LAT, LAT), :] = moved
+                kept[pl.ds(pl.multiple_of((lon * OUTV + v) * LAT, LAT), LAT), :] = moved
+        return carry
+
+    lax.fori_loop(0, LON, one, 0)
     for v in range(WORDS):
         rows = jnp.dot(one_hot, feats[:, v * LEV : (v + 1) * LEV], preferred_element_type=F32)
         outbound[v] = rows.astype(BF16).reshape(PEERS, 2, LEV)
@@ -156,9 +152,7 @@
     return (lax.div(tile, NZ), lax.rem(tile, NZ), lat), emu, tile * NX + lat
 
 
-def greet_all(me, emu):
-    barrier = pltpu.get_barrier_semaphore()
-
+def greet_all(barrier, me, emu):
     def one(index, carry):
         tile_to, lat_to = place(lax.rem(index, PLANE), lax.div(index, PLANE), me)
         pl.semaphore_signal(
@@ -167,7 +161,6 @@
         return carry
 
     lax.fori_loop(1, PEERS, one, 0)
-    pl.semaphore_wait(barrier, PEERS - 1)
 
 
 def z_of(index):
@@ -188,14 +181,28 @@
 
 
 def exchange_kernel(
-    outbound, w_in, b_in, land_vec, w_hid, b_hid, w_out, returned,
-    inbound, answers, go_send, go_recv, back_send, back_recv, own_sem,
+    state, halos, diff, wind, land, route, count,
+    w_in_hbm, b_in, land_vec, w_hid_hbm, b_hid, w_out_hbm, returned, kept,
+    outbound, inbound, answers, feats, sides, w_in, w_hid, w_out,
+    go_send, go_recv, back_send, back_recv, own_sem, weight_sem,
 ):
     me, emu, expert = position()
     own_slot = PEERS - PLANE
+    barrier = pltpu.get_barrier_semaphore()
+    greet_all(barrier, me, emu)
+    weights = [
+        pltpu.make_async_copy(w_in_hbm, w_in, weight_sem.at[0]),
+        pltpu.make_async_copy(w_hid_hbm, w_hid, weight_sem.at[1]),
+        pltpu.make_async_copy(w_out_hbm, w_out, weight_sem.at[2]),
+    ]
+    for copy in weights:
+        copy.start()
+    advance(
+        state, halos, diff, wind, land, route, count, me[2], emu, outbound, kept, feats, sides
+    )
     own = pltpu.make_async_copy(outbound.at[:, expert], inbound.at[:, own_slot], own_sem.at[0])
     own.start()
-    greet_all(me, emu)
+    pl.semaphore_wait(barrier, PEERS - 1)
 
     def forward(piece, index):
         tile_to, lat_to = place(lax.rem(index, PLANE), z_of(lax.div(index, PLANE)), me)
@@ -236,6 +243,9 @@
         start_all(forward, piece, first, last)
     for piece, (first, last) in enumerate(PIECES):
         finish(outbound, inbound, go_send, go_recv, piece, first, last)
+        if piece == 0:
+            for copy in weights:
+                copy.wait()
         if first <= own_slot < last:
             own.wait()
         span = slice(first, last)
@@ -301,24 +311,26 @@
         scratch_shapes=[dma((4,)), dma((4,))], cost_estimate=cost(10**10, 2 * 10**7),
         compiler_params=remote(0, 4), name="halo",
     )(edges)
-    outbound, kept = pl.pallas_call(
-        step_kernel,
-        out_shape=(features, jax.ShapeDtypeStruct((LON * OUTV * LAT, LEV), F32)),
-        in_specs=[vmem, vmem, vmem, vmem, vmem, vmem, smem], out_specs=(vmem, vmem),
-        scratch_shapes=[pltpu.VMEM((COLS, WORDS * LEV), BF16)], cost_estimate=cost(10**10, 2 * 10**7),
-        compiler_params=local(8), name="step",
-    )(flat_state, halos, diff, wind, land, route, count)
-    returned = pl.pallas_call(
-        exchange_kernel, out_shape=answer,
-        in_specs=[anywhere] + [vmem] * 6, out_specs=anywhere,
+    held = [pltpu.with_memory_space_constraint(w[0], pltpu.HBM) for w in (w_in, w_hid, w_out)]
+    returned, kept = pl.pallas_call(
+        exchange_kernel,
+        out_shape=(answer, jax.ShapeDtypeStruct((LON * OUTV * LAT, LEV), F32)),
+        in_specs=[vmem] * 6 + [smem, hbm, vmem, vmem, hbm, vmem, hbm],
+        out_specs=(anywhere, vmem),
         scratch_shapes=[
             pltpu.VMEM(features.shape, BF16),
+            pltpu.VMEM(features.shape, BF16),
             pltpu.VMEM(answer.shape, BF16),
-            dma((2,)), dma((2,)), dma((2,)), dma((2,)), dma((2,)),
+            pltpu.VMEM((COLS, WORDS * LEV), BF16),
+            pltpu.VMEM((2, ROWS, LEV), F32),
+            pltpu.VMEM(held[0].shape, BF16),
+            pltpu.VMEM(held[1].shape, BF16),
+            pltpu.VMEM(held[2].shape, BF16),
+            dma((2,)), dma((2,)), dma((2,)), dma((2,)), dma((2,)), dma((3,)),
         ],
         cost_estimate=cost(2 * 10**9, 10**7),
-        compiler_params=remote(1, 20), name="exchange",
-    )(outbound, w_in[0], b_in, land_vec, w_hid[0], b_hid[0], w_out[0])
+        compiler_params=remote(1, 32), name="exchange",
+    )(flat_state, halos, diff, wind, land, route, count, held[0], b_in, land_vec, held[1], b_hid[0], held[2])
     out = pl.pallas_call(
         combine_kernel,
         out_shape=jax.ShapeDtypeStruct((COLS * OUTV, LEV), F32),

time: 59.7 us -> 56.3 us (0.943)
  Pallas kernels: 57.5 us -> 55.5 us
  local copies, waits for them, and re-layouts: 1.31 us -> 0.02 us
    pallas_call x2 -> x1, Pallas kernels: 41.5 us -> 39.5 us  [body(): pl.pallas_call(exchange_kernel, out_shape=(answer, jax.ShapeDtypeStruct((...]
    unnamed x12 -> x6, local copies, waits for them, and re-layouts: 1.31 us -> 0.02 us
where the time goes in v3:
time: 56.3 us; the launch traced here: 56.2 us
  Pallas kernels  55.5 us (99%)
  between operations  0.72 us (1%)
    pallas_call x1, Pallas kernels, body(): pl.pallas_call(exchange_kernel, out_shape=(answer, jax.ShapeDtypeStruct((...  39.5 us
    pallas_call x1, Pallas kernels, body(): pl.pallas_call(halo_kernel, out_shape=edge, in_specs=[anywhere], out_spec...  13.2 us
    pallas_call x1, Pallas kernels, body(): pl.pallas_call(prepare_kernel, out_shape=[edge] + loaded, in_specs=[hbm]...  1.56 us
    pallas_call x1, Pallas kernels, body(): pl.pallas_call(combine_kernel, out_shape=jax.ShapeDtypeStruct((COLS * OUT...  1.25 us

profile of v3, /device:TPU:1, one launch (start us, length us, event | category | flops | bytes accessed | tf_op | source)
XLA Modules:
  0.0 56.2 jit_solution(11414197449842508460)
XLA Ops:
  0.7 1.6 %prepare.1 = (bf16[4,192,128]{2,1,0:T(8,128)(2,1)S(1)}, f32[3072,128]{1,0:T(8,128)S(1)}, f32[12,128]{1,0:T(8,128)S(1)}, f32[16,16]{1,0:T(8,128)S(1)}, s32[16,16]{1,0:T(8,128)S(1)}, /*index=5*/s32[1,256]{1,0:T(1,128)S(1)}) custom-call(f32[3072,128]{1,0:T(8,128)} %bitcast.15, f32[12,128]{1,0:T(8,128)} %diff.1, f32[16,16]{1,0:T(8,128)} %wind.1, s32[16,16]{1,0:T(8,128)} %land.1, ...), custom_call_target="tpu_custom_call" | custom-call | flops 10000000 | bytes 2000000 | tf_op jit(solution)/shard_map/prepare/pallas_call | solution.py:304
  2.2 0.0 copy-start
  2.2 0.0 copy-start.1
  2.2 0.0 copy-start.2
  2.3 13.2 %halo.1.halos = bf16[4,192,128]{2,1,0:T(8,128)(2,1)S(1)} custom-call(bf16[4,192,128]{2,1,0:T(8,128)(2,1)S(1)} %get-tuple-element.14.edges), custom_call_target="tpu_custom_call" | custom-call | flops 10000000000 | bytes 20000000 | tf_op jit(solution)/shard_map/halo/pallas_call | solution.py:309
  15.5 0.0 copy-done
  15.5 0.0 copy-done.1
  15.5 0.0 copy-done.2
  15.5 39.5 %exchange.1 = (bf16[4,128,2,128]{3,2,1,0:T(2,128)(2,1)S(1)}, f32[1024,128]{1,0:T(8,128)S(1)}) custom-call(f32[3072,128]{1,0:T(8,128)S(1)} %get-tuple-element.13.state, bf16[4,192,128]{2,1,0:T(8,128)(2,1)S(1)} %halo.1.halos, f32[12,128]{1,0:T(8,128)S(1)} %get-tuple-element.15.diff, f32[16,16]{1,0:T(8,128)S(1)} %get-tuple-element.16.wind, ...), custom_call_target="tpu_custom_call" | custom-call | flops 2000000000 | bytes 10000000 | tf_op jit(solution)/shard_map/exchange/pallas_call | solution.py:315
  55.0 1.3 %combine.1 = f32[1024,128]{1,0:T(8,128)} custom-call(bf16[4,128,2,128]{3,2,1,0:T(2,128)(2,1)S(1)} %get-tuple-element.19.returned, f32[1024,128]{1,0:T(8,128)S(1)} %get-tuple-element.20.kept, s32[1,256]{1,0:T(1,128)S(1)} %get-tuple-element.18.route, s32[1,1]{1,0:T(1,128)} %bitcast.11.count), custom_call_target="tpu_custom_call" | custom-call | tf_op jit(solution)/shard_map/combine/pallas_call | solution.py:334
Async XLA Ops:
  2.2 13.2 %copy-start = (f32[1,2,1024]{2,1,0:T(2,128)S(1)}, f32[1,2,1024]{2,1,0:T(2,128)}, u32[]{:S(2)}) copy-start(f32[1,2,1024]{2,1,0:T(2,128)} %param.22) | copy-start | bytes 24580
  2.2 13.2 %copy-start.1 = (f32[1,1024]{1,0:T(1,128)S(1)}, f32[1,1024]{1,0:T(1,128)}, u32[]{:S(2)}) copy-start(f32[1,1024]{1,0:T(1,128)} %b_in.1) | copy-start | bytes 12292
  2.2 13.2 %copy-start.2 = (f32[1,1024]{1,0:T(1,128)S(1)}, f32[1,1024]{1,0:T(1,128)}, u32[]{:S(2)}) copy-start(f32[1,1024]{1,0:T(1,128)} %land_vec.1) | copy-start | bytes 12292

commit v4 on v3

--- a/solution.py
+++ b/solution.py
@@ -64,53 +64,7 @@
     return jnp.broadcast_to(jnp.sum(picked, axis=1, keepdims=True), (LAT, width))
 
 
-def prepare_kernel(
-    state, diff, wind, land, route,
-    edges, state_out, diff_out, wind_out, land_out, route_out, sems,
-):
-    copies = [
-        pltpu.make_async_copy(source, target, sems.at[k])
-        for k, (source, target) in enumerate(
-            ((state, state_out), (diff, diff_out), (wind, wind_out), (land, land_out), (route, route_out))
-        )
-    ]
-    for copy in copies:
-        copy.start()
-    for copy in copies:
-        copy.wait()
-    edges[0] = state_out[pl.ds((LON - 1) * ROWS, ROWS), :].astype(BF16)
-    edges[1] = state_out[pl.ds(0, ROWS), :].astype(BF16)
-    edges[2] = state_out[pl.ds(LAT - 1, LON * VARS, stride=LAT), :].astype(BF16)
-    edges[3] = state_out[pl.ds(0, LON * VARS, stride=LAT), :].astype(BF16)
-
-
-def halo_kernel(edges, halos, send_sem, recv_sem):
-    tile, lat, emu = lax.axis_index("tile"), lax.axis_index("lat"), lax.axis_index("emu")
-    barrier = pltpu.get_barrier_semaphore()
-    tiles = NZ * NY
-    east = (lax.rem(tile + 1, tiles), lat, emu)
-    west = (lax.rem(tile + tiles - 1, tiles), lat, emu)
-    other = (tile, lat, 1 - emu)
-    across = (tile, lax.rem(lat + NX - 1 + 2 * emu, NX), 1 - emu)
-    for device in (east, west, other, across):
-        pl.semaphore_signal(barrier, inc=1, device_id=device, device_id_type=MESH)
-    pl.semaphore_wait(barrier, 4)
-    copies = []
-    for k, (edge, device) in enumerate(((0, east), (1, west), (2 + emu, other), (3 - emu, across))):
-        copy = pltpu.make_async_remote_copy(
-            src_ref=edges.at[edge], dst_ref=halos.at[edge], send_sem=send_sem.at[k],
-            recv_sem=recv_sem.at[k], device_id=device, device_id_type=MESH,
-        )
-        copy.start()
-        copies.append(copy)
-    for copy in copies:
-        copy.wait()
-
-
-def advance(
-    state, halos, diff, wind, land, route, count, lat, emu, outbound, kept, feats, sides,
-):
-    one_hot = slot_matrix(route[...].astype(F32), count[0, 0])
+def advance(state, halos, diff, wind, land, one_hot, lat, emu, outbound, kept, feats, sides):
     sub = lax.broadcasted_iota(jnp.int32, (LAT, LEV), 0)
     sides[0] = halos[2].astype(F32) * jnp.where((lat == 0) & (emu == 0), 0.0, 1.0).astype(F32)
     sides[1] = halos[3].astype(F32) * jnp.where((lat == NX - 1) & (emu == 1), 0.0, 1.0).astype(F32)
@@ -143,24 +97,13 @@
 
     lax.fori_loop(0, LON, one, 0)
     for v in range(WORDS):
-        rows = jnp.dot(one_hot, feats[:, v * LEV : (v + 1) * LEV], preferred_element_type=F32)
+        rows = jnp.dot(one_hot[...], feats[:, v * LEV : (v + 1) * LEV], preferred_element_type=F32)
         outbound[v] = rows.astype(BF16).reshape(PEERS, 2, LEV)
 
 
 def position():
     tile, lat, emu = lax.axis_index("tile"), lax.axis_index("lat"), lax.axis_index("emu")
     return (lax.div(tile, NZ), lax.rem(tile, NZ), lat), emu, tile * NX + lat
-
-
-def greet_all(barrier, me, emu):
-    def one(index, carry):
-        tile_to, lat_to = place(lax.rem(index, PLANE), lax.div(index, PLANE), me)
-        pl.semaphore_signal(
-            barrier, inc=1, device_id=(tile_to, lat_to, emu), device_id_type=MESH
-        )
-        return carry
-
-    lax.fori_loop(1, PEERS, one, 0)
 
 
 def z_of(index):
@@ -181,28 +124,75 @@
 
 
 def exchange_kernel(
-    state, halos, diff, wind, land, route, count,
-    w_in_hbm, b_in, land_vec, w_hid_hbm, b_hid, w_out_hbm, returned, kept,
-    outbound, inbound, answers, feats, sides, w_in, w_hid, w_out,
-    go_send, go_recv, back_send, back_recv, own_sem, weight_sem,
+    state_hbm, diff_hbm, wind_hbm, land_hbm, route_hbm, count,
+    w_in_hbm, b_in_hbm, land_vec_hbm, w_hid_hbm, b_hid_hbm, w_out_hbm, returned, kept,
+    state, diff, wind, land, route, edges, halos, one_hot,
+    outbound, inbound, answers, feats, sides, w_in, b_in, land_vec, w_hid, b_hid, w_out,
+    edge_send, edge_recv, go_send, go_recv, back_send, back_recv, own_sem, load_sem, weight_sem,
+    plane_sem, all_sem,
 ):
     me, emu, expert = position()
+    y, z, lat = me
+    tile, tiles = y * NZ + z, NY * NZ
     own_slot = PEERS - PLANE
+
+    east = (lax.rem(tile + 1, tiles), lat, emu)
+    west = (lax.rem(tile + tiles - 1, tiles), lat, emu)
+    other = (tile, lat, 1 - emu)
+    across = (tile, lax.rem(lat + NX - 1 + 2 * emu, NX), 1 - emu)
+    x_line = [(tile, lax.rem(lat + d, NX), emu) for d in range(1, NX)]
+    y_line = [(lax.rem(y + d, NY) * NZ + z, lat, emu) for d in range(1, NY)]
+    z_line = [(y * NZ + lax.rem(z + d, NZ), lat, emu) for d in range(1, NZ)]
+    greeted = [east, west, other, across] + x_line + y_line + z_line
     barrier = pltpu.get_barrier_semaphore()
-    greet_all(barrier, me, emu)
-    weights = [
-        pltpu.make_async_copy(w_in_hbm, w_in, weight_sem.at[0]),
-        pltpu.make_async_copy(w_hid_hbm, w_hid, weight_sem.at[1]),
-        pltpu.make_async_copy(w_out_hbm, w_out, weight_sem.at[2]),
-    ]
-    for copy in weights:
+    for device in greeted:
+        pl.semaphore_signal(barrier, inc=1, device_id=device, device_id_type=MESH)
+
+    def copies_of(pairs, sems):
+        made = [pltpu.make_async_copy(a, b, sems.at[k]) for k, (a, b) in enumerate(pairs)]
+        for copy in made:
+            copy.start()
+        return made
+
+    loads = copies_of(
+        ((state_hbm, state), (diff_hbm, diff), (wind_hbm, wind), (land_hbm, land), (route_hbm, route)),
+        load_sem,
+    )
+    weights = copies_of(
+        (
+            (w_in_hbm, w_in), (b_in_hbm, b_in), (land_vec_hbm, land_vec),
+            (w_hid_hbm, w_hid), (b_hid_hbm, b_hid), (w_out_hbm, w_out),
+        ),
+        weight_sem,
+    )
+    for copy in loads:
+        copy.wait()
+
+    edges[0] = state[pl.ds((LON - 1) * ROWS, ROWS), :].astype(BF16)
+    edges[1] = state[pl.ds(0, ROWS), :].astype(BF16)
+    edges[2] = state[pl.ds(LAT - 1, LON * VARS, stride=LAT), :].astype(BF16)
+    edges[3] = state[pl.ds(0, LON * VARS, stride=LAT), :].astype(BF16)
+    pl.semaphore_wait(barrier, len(greeted))
+    sent = []
+    for k, (edge, device) in enumerate(((0, east), (1, west), (2 + emu, other), (3 - emu, across))):
+        copy = pltpu.make_async_remote_copy(
+            src_ref=edges.at[edge], dst_ref=halos.at[edge], send_sem=edge_send.at[k],
+            recv_sem=edge_recv.at[k], device_id=device, device_id_type=MESH,
+        )
         copy.start()
-    advance(
-        state, halos, diff, wind, land, route, count, me[2], emu, outbound, kept, feats, sides
-    )
+        sent.append(copy)
+    for device in y_line:
+        pl.semaphore_signal(plane_sem, inc=1, device_id=device, device_id_type=MESH)
+    one_hot[...] = slot_matrix(route[...].astype(F32), count[0, 0])
+    pl.semaphore_wait(plane_sem, len(y_line))
+    for device in z_line:
+        pl.semaphore_signal(all_sem, inc=1, device_id=device, device_id_type=MESH)
+    for copy in sent:
+        copy.wait()
+    advance(state, halos, diff, wind, land, one_hot, lat, emu, outbound, kept, feats, sides)
     own = pltpu.make_async_copy(outbound.at[:, expert], inbound.at[:, own_slot], own_sem.at[0])
     own.start()
-    pl.semaphore_wait(barrier, PEERS - 1)
+    pl.semaphore_wait(all_sem, len(z_line))
 
     def forward(piece, index):
         tile_to, lat_to = place(lax.rem(index, PLANE), z_of(lax.div(index, PLANE)), me)
@@ -285,52 +275,45 @@
     hbm = pl.BlockSpec(memory_space=pltpu.HBM)
     anywhere = pl.BlockSpec(memory_space=pl.ANY)
     dma = pltpu.SemaphoreType.DMA
-    edge = jax.ShapeDtypeStruct((4, ROWS, LEV), BF16)
     features = jax.ShapeDtypeStruct((WORDS, PEERS, 2, LEV), BF16)
     answer = jax.ShapeDtypeStruct((OUTV, PEERS, 2, LEV), BF16)
-    loaded = [jax.ShapeDtypeStruct(x.shape, x.dtype) for x in (flat_state, diff, wind, land, route)]
-
-    def remote(number, size):
-        return pltpu.CompilerParams(
-            collective_id=number, has_side_effects=True, vmem_limit_bytes=size << 20
-        )
 
     def local(size):
         return pltpu.CompilerParams(vmem_limit_bytes=size << 20)
 
-    def cost(flops, size):
-        return pl.CostEstimate(flops=flops, bytes_accessed=size, transcendentals=0)
-
-    edges, flat_state, diff, wind, land, route = pl.pallas_call(
-        prepare_kernel, out_shape=[edge] + loaded, in_specs=[hbm] * 5, out_specs=[vmem] * 6,
-        scratch_shapes=[dma((5,))], cost_estimate=cost(10**7, 2 * 10**6),
-        compiler_params=local(4), name="prepare",
-    )(*[pltpu.with_memory_space_constraint(x, pltpu.HBM) for x in (flat_state, diff, wind, land, route)])
-    halos = pl.pallas_call(
-        halo_kernel, out_shape=edge, in_specs=[anywhere], out_specs=anywhere,
-        scratch_shapes=[dma((4,)), dma((4,))], cost_estimate=cost(10**10, 2 * 10**7),
-        compiler_params=remote(0, 4), name="halo",
-    )(edges)
-    held = [pltpu.with_memory_space_constraint(w[0], pltpu.HBM) for w in (w_in, w_hid, w_out)]
+    def held(*arrays):
+        return [pltpu.with_memory_space_constraint(x, pltpu.HBM) for x in arrays]
+
+    inputs = held(flat_state, diff, wind, land, route)
+    params = held(w_in[0], b_in, land_vec, w_hid[0], b_hid[0], w_out[0])
     returned, kept = pl.pallas_call(
         exchange_kernel,
         out_shape=(answer, jax.ShapeDtypeStruct((LON * OUTV * LAT, LEV), F32)),
-        in_specs=[vmem] * 6 + [smem, hbm, vmem, vmem, hbm, vmem, hbm],
+        in_specs=[hbm] * 5 + [smem] + [hbm] * 6,
         out_specs=(anywhere, vmem),
-        scratch_shapes=[
+        scratch_shapes=[pltpu.VMEM(x.shape, x.dtype) for x in inputs]
+        + [
+            pltpu.VMEM((4, ROWS, LEV), BF16),
+            pltpu.VMEM((4, ROWS, LEV), BF16),
+            pltpu.VMEM((COLS, COLS), BF16),
             pltpu.VMEM(features.shape, BF16),
             pltpu.VMEM(features.shape, BF16),
             pltpu.VMEM(answer.shape, BF16),
             pltpu.VMEM((COLS, WORDS * LEV), BF16),
             pltpu.VMEM((2, ROWS, LEV), F32),
-            pltpu.VMEM(held[0].shape, BF16),
-            pltpu.VMEM(held[1].shape, BF16),
-            pltpu.VMEM(held[2].shape, BF16),
-            dma((2,)), dma((2,)), dma((2,)), dma((2,)), dma((2,)), dma((3,)),
+        ]
+        + [pltpu.VMEM(x.shape, x.dtype) for x in params]
+        + [
+            dma((4,)), dma((4,)), dma((2,)), dma((2,)), dma((2,)), dma((2,)), dma((2,)),
+            dma((5,)), dma((6,)),
+            pltpu.SemaphoreType.REGULAR, pltpu.SemaphoreType.REGULAR,
         ],
-        cost_estimate=cost(2 * 10**9, 10**7),
-        compiler_params=remote(1, 32), name="exchange",
-    )(flat_state, halos, diff, wind, land, route, count, held[0], b_in, land_vec, held[1], b_hid[0], held[2])
+        cost_estimate=pl.CostEstimate(flops=2 * 10**10, bytes_accessed=10**7, transcendentals=0),
+        compiler_params=pltpu.CompilerParams(
+            collective_id=0, has_side_effects=True, vmem_limit_bytes=36 << 20
+        ),
+        name="exchange",
+    )(*inputs, count, *params)
     out = pl.pallas_call(
         combine_kernel,
         out_shape=jax.ShapeDtypeStruct((COLS * OUTV, LEV), F32),

time: 56.3 us -> 52.1 us (0.925)
  Pallas kernels: 55.5 us -> 51.4 us
    pallas_call x2 -> x0, Pallas kernels: 14.7 us -> none  [the longest x1 13.2 us: body(): pl.pallas_call(halo_kernel, out_shape=edge, in_specs=[anywhere], out_spec...]
    pallas_call x1, Pallas kernels: 39.5 us -> 50.1 us  [body(): pl.pallas_call(exchange_kernel, out_shape=(answer, jax.ShapeDtypeStruct((...]
where the time goes in v4:
time: 52.1 us; the launch traced here: 52 us
  Pallas kernels  51.4 us (99%)
  between operations  0.68 us (1%)
    pallas_call x1, Pallas kernels, body(): pl.pallas_call(exchange_kernel, out_shape=(answer, jax.ShapeDtypeStruct((...  50.1 us
    pallas_call x1, Pallas kernels, body(): pl.pallas_call(combine_kernel, out_shape=jax.ShapeDtypeStruct((COLS * OUT...  1.25 us

profile of v4, /device:TPU:1, one launch (start us, length us, event | category | flops | bytes accessed | tf_op | source)
XLA Modules:
  0.0 52.0 jit_solution(565891530848872122)
XLA Ops:
  0.7 0.0 copy-start
  0.7 50.1 %exchange.1 = (bf16[4,128,2,128]{3,2,1,0:T(2,128)(2,1)S(1)}, f32[1024,128]{1,0:T(8,128)S(1)}) custom-call(f32[3072,128]{1,0:T(8,128)} %bitcast.16, f32[12,128]{1,0:T(8,128)} %diff_hbm.1, f32[16,16]{1,0:T(8,128)} %wind_hbm.1, s32[16,16]{1,0:T(8,128)} %land_hbm.1, s32[1,256]{1,0:T(1,128)} %bitcast.12, s32[1,1]{1,0:T(1,128)} %bitcast.10.count, ...), custom_call_target="tpu_custom_call" | custom-call | flops 20000000000 | bytes 10000000 | tf_op jit(solution)/shard_map/exchange/pallas_call | solution.py:289
  50.8 0.0 copy-done
  50.8 1.2 %combine.1 = f32[1024,128]{1,0:T(8,128)} custom-call(bf16[4,128,2,128]{3,2,1,0:T(2,128)(2,1)S(1)} %get-tuple-element.7.returned, f32[1024,128]{1,0:T(8,128)S(1)} %get-tuple-element.8.kept, s32[1,256]{1,0:T(1,128)S(1)} %bitcast.13, s32[1,1]{1,0:T(1,128)} %bitcast.11.count), custom_call_target="tpu_custom_call" | custom-call | tf_op jit(solution)/shard_map/combine/pallas_call | solution.py:317
Async XLA Ops:
  0.7 50.1 %copy-start = (s32[1,1,1,256,1]{3,4,2,1,0:T(1,128)S(1)}, s32[1,1,1,256,1]{3,4,2,1,0:T(1,128)}, u32[]{:S(2)}) copy-start(s32[1,1,1,256,1]{3,4,2,1,0:T(1,128)} %param.16) | copy-start | bytes 3076

commit v5 on v4

--- a/solution.py
+++ b/solution.py
@@ -21,7 +21,7 @@
 WORDS = VARS + 1
 
 
-PIECES = ((0, 80), (80, 128))
+PIECES = ((0, 48), (48, 80), (80, 128))
 
 
 def place(step, z_off, me):
@@ -304,7 +304,7 @@
         ]
         + [pltpu.VMEM(x.shape, x.dtype) for x in params]
         + [
-            dma((4,)), dma((4,)), dma((2,)), dma((2,)), dma((2,)), dma((2,)), dma((2,)),
+            dma((4,)), dma((4,)), dma((3,)), dma((3,)), dma((3,)), dma((3,)), dma((2,)),
             dma((5,)), dma((6,)),
             pltpu.SemaphoreType.REGULAR, pltpu.SemaphoreType.REGULAR,
         ],

time: 52.1 us -> 49.6 us (0.952)
  Pallas kernels: 51.4 us -> 48.8 us
    pallas_call x1, Pallas kernels: 50.1 us -> 47.5 us  [body(): pl.pallas_call(exchange_kernel, out_shape=(answer, jax.ShapeDtypeStruct((...]
where the time goes in v5:
time: 49.6 us; the launch traced here: 49.5 us
  Pallas kernels  48.8 us (98%)
  between operations  0.68 us (1%)
    pallas_call x1, Pallas kernels, body(): pl.pallas_call(exchange_kernel, out_shape=(answer, jax.ShapeDtypeStruct((...  47.5 us
    pallas_call x1, Pallas kernels, body(): pl.pallas_call(combine_kernel, out_shape=jax.ShapeDtypeStruct((COLS * OUT...  1.25 us

profile of v5, /device:TPU:1, one launch (start us, length us, event | category | flops | bytes accessed | tf_op | source)
XLA Modules:
  0.0 49.5 jit_solution(16922456236779067583)
XLA Ops:
  0.7 0.0 copy-start
  0.7 47.5 %exchange.1 = (bf16[4,128,2,128]{3,2,1,0:T(2,128)(2,1)S(1)}, f32[1024,128]{1,0:T(8,128)S(1)}) custom-call(f32[3072,128]{1,0:T(8,128)} %bitcast.16, f32[12,128]{1,0:T(8,128)} %diff_hbm.1, f32[16,16]{1,0:T(8,128)} %wind_hbm.1, s32[16,16]{1,0:T(8,128)} %land_hbm.1, s32[1,256]{1,0:T(1,128)} %bitcast.12, s32[1,1]{1,0:T(1,128)} %bitcast.10.count, ...), custom_call_target="tpu_custom_call" | custom-call | flops 20000000000 | bytes 10000000 | tf_op jit(solution)/shard_map/exchange/pallas_call | solution.py:289
  48.2 0.0 copy-done
  48.2 1.3 %combine.1 = f32[1024,128]{1,0:T(8,128)} custom-call(bf16[4,128,2,128]{3,2,1,0:T(2,128)(2,1)S(1)} %get-tuple-element.7.returned, f32[1024,128]{1,0:T(8,128)S(1)} %get-tuple-element.8.kept, s32[1,256]{1,0:T(1,128)S(1)} %bitcast.13, s32[1,1]{1,0:T(1,128)} %bitcast.11.count), custom_call_target="tpu_custom_call" | custom-call | tf_op jit(solution)/shard_map/combine/pallas_call | solution.py:317
Async XLA Ops:
  0.7 47.6 %copy-start = (s32[1,1,1,256,1]{3,4,2,1,0:T(1,128)S(1)}, s32[1,1,1,256,1]{3,4,2,1,0:T(1,128)}, u32[]{:S(2)}) copy-start(s32[1,1,1,256,1]{3,4,2,1,0:T(1,128)} %param.16) | copy-start | bytes 3076
